TPU v7x, 32 devices: a 4x4x1 block of a 4x4x8 slice. The times are simulated.
32 devices in a mesh: dp: 1 (over z), tp: 4 (over y), ep: 8 (over x, core).
Axes of the slice: x: 4, y: 4, z: 1, core: 2. Of those that a mesh axis runs over, the one named last changes fastest.
The devices are a block of a 4x4x8 slice.
Arguments:
- hidden_in: bfloat16 [128, 256, 768], P(('dp', 'ep'), 'tp')
- ln_attn: float32 [2, 768], replicated
- ln_ffn: float32 [2, 768], replicated
- w_query: bfloat16 [2, 768, 768], P(None, None, 'tp')
- w_key: bfloat16 [2, 768, 768], P(None, None, 'tp')
- w_value: bfloat16 [2, 768, 768], P(None, None, 'tp')
- w_out: bfloat16 [2, 768, 768], P(None, 'tp')
- bias_table: float32 [2, 12, 32], P(None, 'tp')
- w_gate: bfloat16 [768, 3072], P(None, 'tp')
- w_up: bfloat16 [768, 3072], P(None, 'tp')
- w_down: bfloat16 [3072, 768], P('tp')
- w_router: float32 [768, 128], replicated
- expert_in: bfloat16 [128, 768, 3072], P(('tp', 'ep'))
- expert_out: bfloat16 [128, 3072, 768], P(('tp', 'ep'))
- expert_ids: int32 [128, 256, 2], P(('dp', 'ep'), 'tp')
Outputs:
- output 1: bfloat16 [128, 256, 768], P(('dp', 'ep'), 'tp')
- output 2: bfloat16 [2, 128, 12, 256, 64], P(None, ('dp', 'ep'), 'tp')
- output 3: bfloat16 [2, 128, 12, 256, 64], P(None, ('dp', 'ep'), 'tp')
All inputs are finite; a program needn't handle non-finite values.
Results may differ from a plain program's by a relative error of at most 0.0120554.
Values are sent between devices in bfloat16 or wider.
A program may use at most 768 MiB of HBM per device.

v0:
```python
import jax
import jax.numpy as jnp
from jax import lax
from jax.sharding import PartitionSpec as P

EXACT_BUCKETS = 16
THRESHOLDS = (18, 20, 23, 26, 30, 34, 39, 45, 51, 58, 66, 76, 86, 98, 112)
EPSILON = 1e-6


def bucket_of(rel_pos):
    bucket_idx = jnp.minimum(rel_pos, EXACT_BUCKETS)
    for threshold in THRESHOLDS:
        bucket_idx = bucket_idx + (rel_pos >= threshold).astype(jnp.int32)
    return bucket_idx


def rms_norm(rows_in, ln_scale):
    wide_rows = rows_in.astype(jnp.float32)
    inv_rms = lax.rsqrt(jnp.mean(wide_rows * wide_rows, axis=-1, keepdims=True) + EPSILON)
    return (wide_rows * inv_rms * ln_scale).astype(jnp.bfloat16)


def causal_bias(bias_rows, seq_len):
    positions = jnp.arange(seq_len)
    rel_pos = positions[:, None] - positions[None, :]
    bias_full = jnp.take(bias_rows, bucket_of(jnp.maximum(rel_pos, 0)), axis=1)
    return jnp.where(rel_pos[None] >= 0, bias_full, -jnp.inf)


def attend(normed_full, w_query, w_key, w_value, bias_rows):
    local_batch, seq_len, d_model = normed_full.shape
    num_heads = bias_rows.shape[0]
    head_dim = w_query.shape[1] // num_heads

    def project(weight):
        projected = jnp.einsum('btd,dk->btk', normed_full, weight, preferred_element_type=jnp.float32)
        return projected.astype(jnp.bfloat16).reshape(local_batch, seq_len, num_heads, head_dim)

    queries = project(w_query)
    keys_full = project(w_key)
    values_full = project(w_value)
    scores = jnp.einsum('bqhd,bkhd->bhqk', queries, keys_full, preferred_element_type=jnp.float32)
    scores = scores * (head_dim ** -0.5) + causal_bias(bias_rows, seq_len)[None]
    attn_probs = jax.nn.softmax(scores, axis=-1).astype(jnp.bfloat16)
    context = jnp.einsum('bhqk,bkhd->bqhd', attn_probs, values_full, preferred_element_type=jnp.float32)
    context = context.astype(jnp.bfloat16).reshape(local_batch, seq_len, num_heads * head_dim)
    return context, jnp.swapaxes(keys_full, 1, 2), jnp.swapaxes(values_full, 1, 2)


def attention_block(hidden, ln_scale, w_query, w_key, w_value, w_out, bias_rows):
    normed = rms_norm(hidden, ln_scale)
    gathered = lax.all_gather(normed, 'tp', axis=1, tiled=True)
    context, keys_cache, values_cache = attend(gathered, w_query, w_key, w_value, bias_rows)
    part_sum = jnp.einsum('crl,le->cre', context, w_out, preferred_element_type=jnp.float32)
    reduced = lax.psum_scatter(part_sum, 'tp', scatter_dimension=1, tiled=True)
    return (hidden.astype(jnp.float32) + reduced).astype(jnp.bfloat16), keys_cache, values_cache


def ffn_block(hidden, ln_scale, w_gate, w_up, w_down):
    normed = rms_norm(hidden, ln_scale)
    gathered = lax.all_gather(normed, 'tp', axis=1, tiled=True)
    gate_pre = jnp.einsum('btd,df->btf', gathered, w_gate, preferred_element_type=jnp.float32)
    up_pre = jnp.einsum('btd,df->btf', gathered, w_up, preferred_element_type=jnp.float32)
    ffn_hidden = (jax.nn.gelu(gate_pre) * up_pre).astype(jnp.bfloat16)
    part_sum = jnp.einsum('btf,fd->btd', ffn_hidden, w_down, preferred_element_type=jnp.float32)
    reduced = lax.psum_scatter(part_sum, 'tp', scatter_dimension=1, tiled=True)
    return (hidden.astype(jnp.float32) + reduced).astype(jnp.bfloat16)


def slot_table(choices, num_experts):
    experts = jnp.arange(num_experts, dtype=jnp.int32)
    first_hot = (choices[..., 0:1] == experts).astype(jnp.int32)
    second_hot = (choices[..., 1:2] == experts).astype(jnp.int32)
    first_pos = jnp.sum((jnp.cumsum(first_hot, axis=-2) - 1) * first_hot, axis=-1)
    second_base = jnp.cumsum(second_hot, axis=-2) - 1 + jnp.sum(first_hot, axis=-2, keepdims=True)
    second_pos = jnp.sum(second_base * second_hot, axis=-1)
    return jnp.stack([first_pos, second_pos], axis=-1)


def route(normed, choices, w_router, num_experts, capacity):
    logits = jnp.dot(normed.astype(jnp.float32), w_router, precision=lax.Precision.HIGHEST)
    router_probs = jax.nn.softmax(logits, axis=-1)
    picked = jnp.take_along_axis(router_probs, choices, axis=-1)
    gate_weights = picked / jnp.sum(picked, axis=-1, keepdims=True)
    position = slot_table(choices, num_experts)
    slot_ids = jnp.where(position < capacity, choices * capacity + position, -1)
    columns = jnp.arange(num_experts * capacity, dtype=jnp.int32)
    select = (slot_ids[:, :, None] == columns).astype(jnp.bfloat16)
    return gate_weights, select


def moe_block(hidden, ln_scale, w_router, expert_in, expert_out, expert_ids):
    local_batch, local_seq, d_model = hidden.shape
    tokens = local_batch * local_seq
    num_experts = w_router.shape[1]
    local_experts = expert_in.shape[0]
    groups = num_experts // local_experts
    capacity = 4 * tokens // num_experts
    normed = rms_norm(hidden, ln_scale).reshape(tokens, d_model)
    gate_weights, select = route(normed, expert_ids.reshape(tokens, 2), w_router, num_experts, capacity)
    dispatched = jnp.einsum('ncs,nd->sd', select, normed, preferred_element_type=jnp.float32).astype(jnp.bfloat16)
    dispatched = dispatched.reshape(groups, local_experts, capacity, d_model)
    received = lax.all_to_all(dispatched, ('tp', 'ep'), 0, 2, tiled=True)
    expert_rows = received.reshape(local_experts, groups * capacity, d_model)
    expert_hidden = jnp.einsum('erd,edf->erf', expert_rows, expert_in, preferred_element_type=jnp.float32)
    expert_hidden = jax.nn.gelu(expert_hidden).astype(jnp.bfloat16)
    expert_result = jnp.einsum('erf,efd->erd', expert_hidden, expert_out, preferred_element_type=jnp.float32).astype(jnp.bfloat16)
    expert_result = expert_result.reshape(1, local_experts, groups * capacity, d_model)
    returned = lax.all_to_all(expert_result, ('tp', 'ep'), 2, 0, tiled=True)
    returned = returned.reshape(num_experts * capacity, d_model)
    gathered_out = jnp.einsum('ncs,sd->ncd', select, returned, preferred_element_type=jnp.float32)
    moe_sum = jnp.sum(gate_weights[:, :, None] * gathered_out, axis=1).reshape(local_batch, local_seq, d_model)
    return (hidden.astype(jnp.float32) + moe_sum).astype(jnp.bfloat16)


def solution(mesh):
    act_spec = P(('dp', 'ep'), 'tp', None)
    col_spec = P(None, None, 'tp')
    row_spec = P(None, 'tp', None)
    expert_spec = P(('tp', 'ep'), None, None)
    cache_spec = P(None, ('dp', 'ep'), 'tp', None, None)
    in_specs = (act_spec, P(), P(), col_spec, col_spec, col_spec, row_spec, row_spec,
                P(None, 'tp'), P(None, 'tp'), P('tp', None), P(), expert_spec, expert_spec, act_spec)

    def device_fn(hidden_in, ln_attn, ln_ffn, w_query, w_key, w_value, w_out, bias_table, w_gate, w_up, w_down, w_router, expert_in, expert_out, expert_ids):
        hidden, keys_zero, values_zero = attention_block(hidden_in, ln_attn[0], w_query[0], w_key[0], w_value[0], w_out[0], bias_table[0])
        hidden = ffn_block(hidden, ln_ffn[0], w_gate, w_up, w_down)
        hidden, keys_one, values_one = attention_block(hidden, ln_attn[1], w_query[1], w_key[1], w_value[1], w_out[1], bias_table[1])
        hidden = moe_block(hidden, ln_ffn[1], w_router, expert_in, expert_out, expert_ids)
        return hidden, jnp.stack([keys_zero, keys_one]), jnp.stack([values_zero, values_one])

    return jax.shard_map(device_fn, mesh=mesh, in_specs=in_specs, out_specs=(act_spec, cache_spec, cache_spec), check_vma=False)
```

profile of v0, /device:TPU:97, one launch (start us, length us, event | category | flops | bytes accessed | tf_op | source)
XLA Modules:
  0.0 1339.2 jit_solution(18175358280859302237)
XLA Ops:
  14.2 215.5 %gather_fusion.1 = f32[65536,3]{1,0:T(8,128)} fusion(f32[3,32]{0,1:T(8,128)S(1)} %bitcast.157, s32[65536]{0:T(1024)S(1)} %broadcast_clamp_fusion), kind=kCustom, calls=%fused_computation.clone | custom fusion | bytes 1835008 | tf_op jit(solution)/shard_map/jit(_take)/gather | solution.py:27
  229.7 19.0 %copy.80 = f32[256,256,3]{0,1,2:T(8,128)S(1)} copy(f32[256,256,3]{2,1,0:T(8,128)} %bitcast.160) | data formatting | bytes 1572864 | tf_op jit(solution)/shard_map/jit(_take)/gather | solution.py:27
  248.7 215.5 %gather_fusion.2 = f32[65536,3]{1,0:T(8,128)} fusion(f32[3,32]{0,1:T(8,128)S(1)} %bitcast.158, s32[65536]{0:T(1024)S(1)} %broadcast_clamp_fusion), kind=kCustom, calls=%fused_computation.1.clone | custom fusion | bytes 1835008 | tf_op jit(solution)/shard_map/jit(_take)/gather | solution.py:27
  464.2 19.1 %copy.84 = f32[256,256,3]{0,1,2:T(8,128)S(1)} copy(f32[256,256,3]{2,1,0:T(8,128)} %bitcast.159) | data formatting | bytes 1572864 | tf_op jit(solution)/shard_map/jit(_take)/gather | solution.py:27
  487.2 5.1 convolution_convert_fusion.4
  495.7 10.8 fusion.131
  506.5 5.0 convolution_convert_fusion.6
  511.5 6.5 fusion.56
  518.0 6.4 fusion.79
  525.8 114.6 %reduce-scatter.4.cloned.1.call-done = f32[16,64,768]{2,1,0:T(8,128)} async-done(((f32[16,256,768]{2,1,0:T(8,128)}), f32[16,64,768]{2,1,0:T(8,128)}) %reduce-scatter.4.cloned.1.call-update) | async-done | bytes 3145744 | tf_op jit(solution)/shard_map/reduce_scatter | solution.py:56
  645.7 62.9 %all-gather.6.cloned.1.call-done = bf16[16,256,768]{2,1,0:T(8,128)(2,1)} async-done(((bf16[16,64,768]{2,1,0:T(8,128)(2,1)}), bf16[16,256,768]{2,1,0:T(8,128)(2,1)}) %all-gather.6.cloned.1.call-update) | async-done | bytes 6291472 | tf_op jit(solution)/shard_map/all_gather | solution.py:62
  708.6 10.6 fusion.64
  719.2 19.0 %fusion.33 = f32[16,256,768]{2,1,0:T(8,128)} fusion(f32[16,256,768]{2,1,0:T(8,128)} %fusion.64, bf16[16,256,768]{2,1,0:T(8,128)(2,1)} %all-gather.6.cloned.1.call-done, bf16[768,768]{1,0:T(8,128)(2,1)S(1)} %copy-done.26, bf16[768,768]{1,0:T(8,128)(2,1)} %param.26), kind=kOutput, calls=%fused_computation.49 | convolution fusion | flops 9695133696 | bytes 33816576 | tf_op jit(solution)/shard_map/btf,fd->btd/dot_general | solution.py:66
  738.4 112.7 %reduce-scatter.6.cloned.1.call-done = f32[16,64,768]{2,1,0:T(8,128)} async-done(((f32[16,256,768]{2,1,0:T(8,128)}), f32[16,64,768]{2,1,0:T(8,128)}) %reduce-scatter.6.cloned.1.call-update) | async-done | bytes 3145744 | tf_op jit(solution)/shard_map/reduce_scatter | solution.py:67
  856.1 62.5 %all-gather.8.cloned.1.call-done = bf16[16,256,768]{2,1,0:T(8,128)(2,1)} async-done(((bf16[16,64,768]{2,1,0:T(8,128)(2,1)}), bf16[16,256,768]{2,1,0:T(8,128)(2,1)}) %all-gather.8.cloned.1.call-update) | async-done | bytes 6291472 | tf_op jit(solution)/shard_map/all_gather | solution.py:53
  918.7 6.4 convolution_convert_fusion.1
  925.0 4.3 convolution_convert_fusion.2
  929.3 10.5 fusion.132
  939.9 5.0 convolution_convert_fusion.3
  944.8 6.5 fusion.55
  951.3 6.4 fusion.74
  960.4 14.0 %convert_reduce_fusion = bf16[1024,4096]{1,0:T(8,128)(2,1)} fusion(s32[1024,2]{0,1:T(2,128)S(1)} %compare_select_fusion.4), kind=kLoop, calls=%fused_computation.14 | loop fusion | flops 29360128 | bytes 8396800 | tf_op jit(solution)/shard_map/ncs,nd->sd/reduce_sum | solution.py:102
  974.4 96.3 %reduce-scatter.8.cloned.1.call-done = f32[16,64,768]{2,1,0:T(8,128)} async-done(((f32[16,256,768]{2,1,0:T(8,128)}), f32[16,64,768]{2,1,0:T(8,128)}) %reduce-scatter.8.cloned.1.call-update) | async-done | bytes 3145744 | tf_op jit(solution)/shard_map/reduce_scatter | solution.py:56
  1075.5 8.0 fusion.134
  1083.6 82.4 %all_to_all.30 = bf16[32,4,32,768]{3,2,1,0:T(8,128)(2,1)S(1)} all-to-all(bf16[32,4,32,768]{3,2,1,0:T(8,128)(2,1)S(1)} %bitcast.163), channel_id=1, replica_groups=mesh['dp'=1,'tp'=4,'ep'=8] {'tp','ep'}, dimensions={0} | all-to-all | bytes 12582912 | tf_op jit(solution)/shard_map/all_to_all | solution.py:104
  1169.2 46.5 %convert_bitcast_fusion = bf16[1,4,1024,768]{3,2,1,0:T(8,128)(2,1)} fusion(bf16[4,3072,768]{2,1,0:T(8,128)(2,1)} %param.30, bf16[4,1024,768]{2,1,0:T(8,128)(2,1)} %bitcast.164, bf16[4,768,3072]{2,1,0:T(8,128)(2,1)} %param.29), kind=kOutput, calls=%fused_computation.44 | convolution fusion | flops 38771097600 | bytes 50331648 | tf_op jit(solution)/shard_map/erf,efd->erd/dot_general | solution.py:108
  1215.7 10.3 copy.99
  1226.0 7.3 all-to-all-start.1
  1233.9 4.9 pad_maximum_fusion
  1240.7 16.8 %gather_fusion = f32[2048]{0:T(1024)S(1)} fusion(f32[1024,128]{0,1:T(8,128)S(1)} %fusion.72, s32[2048]{0:T(1024)S(1)} %reshape.296), kind=kCustom, calls=%fused_computation.2 | custom fusion | bytes 32768 | tf_op jit(solution)/shard_map/jit(take_along_axis)/gather | solution.py:84
  1259.0 51.6 %all-to-all-done.1 = bf16[1,4,1024,768]{3,1,0,2:T(4,128)(2,1)} async-done(((bf16[1,4,1024,768]{3,1,0,2:T(4,128)(2,1)}), bf16[1,4,1024,768]{3,1,0,2:T(4,128)(2,1)}, u32[]{:S(2)}, u32[]{:S(2)}) %all-to-all-start.1) | async-done | bytes 6291488 | tf_op jit(solution)/shard_map/all_to_all | solution.py:110
  1314.9 15.3 %multiply_reduce_fusion = f32[1024,768]{1,0:T(8,128)S(1)} fusion(f32[1024,2]{0,1:T(2,128)S(1)} %fusion.112, bf16[4096,768,1]{1,0,2:T(8,128)(2,1)S(1)} %bitcast.162, s32[1024,2]{0,1:T(2,128)S(1)} %copy-done.18), kind=kOutput, calls=%fused_computation.43 | convolution fusion | flops 12895649792 | bytes 9453568 | tf_op jit(solution)/shard_map/ncs,sd->ncd/dot_general | solution.py:112
  (138 shorter events, 46.2 us)
Async XLA Ops:
  7.2 701.4 %copy-start = (bf16[768,768]{1,0:T(8,128)(2,1)S(1)}, bf16[768,768]{1,0:T(8,128)(2,1)}, u32[]{:S(2)}) copy-start(bf16[768,768]{1,0:T(8,128)(2,1)} %param.25) | copy-start | bytes 3538948
  7.2 480.0 %all-gather.4.cloned.1.call-start = ((), (), s32[]{:S(2)}) async-start(), calls=%async_computation.5 | async-start | bytes 7864320 | tf_op jit(solution)/shard_map/all_gather | solution.py:53
  10.4 3.6 copy-start.23
  13.5 626.9 %reduce-scatter.4.cloned.1.call-start = ((), (), s32[]{:S(2)}) async-start(), calls=%async_computation.6 | async-start | bytes 15728640 | tf_op jit(solution)/shard_map/reduce_scatter | solution.py:56
  487.2 5.1 copy-start.24
  487.2 5.1 copy-start.28
  492.4 3.3 copy-start.7
  506.5 5.0 copy-start.30
  511.5 6.5 copy-start.8
  511.5 6.5 copy-start.10
  524.5 115.9 %copy-start.2 = (bf16[16,64,768]{2,1,0:T(8,128)(2,1)S(1)}, bf16[16,64,768]{2,1,0:T(8,128)(2,1)}, u32[]{:S(2)}) copy-start(bf16[16,64,768]{2,1,0:T(8,128)(2,1)} %param.17) | copy-start | bytes 4718596
  524.5 184.1 %all-gather.6.cloned.1.call-start = ((), (), s32[]{:S(2)}) async-start(), calls=%async_computation.7 | async-start | bytes 7864320 | tf_op jit(solution)/shard_map/all_gather | solution.py:62
  640.4 3.6 copy-start.21
  645.6 73.6 %copy-start.26 = (bf16[768,768]{1,0:T(8,128)(2,1)S(1)}, bf16[768,768]{1,0:T(8,128)(2,1)}, u32[]{:S(2)}) copy-start(bf16[768,768]{1,0:T(8,128)(2,1)} %param.27) | copy-start | bytes 3538948
  645.6 205.5 %reduce-scatter.6.cloned.1.call-start = ((), (), s32[]{:S(2)}) async-start(), calls=%async_computation.8 | async-start | bytes 15728640 | tf_op jit(solution)/shard_map/reduce_scatter | solution.py:67
  738.3 115.7 %copy-start.20 = (f32[768]{0:T(1024)S(1)}, f32[768]{0:T(1024)}, u32[]{:S(2)}) copy-start(f32[768]{0:T(1024)} %get-tuple-element.6) | copy-start | bytes 9220
  738.3 180.4 %all-gather.8.cloned.1.call-start = ((), (), s32[]{:S(2)}) async-start(), calls=%async_computation.9 | async-start | bytes 7864320 | tf_op jit(solution)/shard_map/all_gather | solution.py:53
  854.0 64.7 %copy-start.27 = (bf16[2,768,192]{1,2,0:T(8,128)(2,1)S(1)}, bf16[2,768,192]{1,2,0:T(8,128)(2,1)}, u32[]{:S(2)}) copy-start(bf16[2,768,192]{1,2,0:T(8,128)(2,1)} %param.21) | copy-start | bytes 1769476
  855.6 215.0 %reduce-scatter.8.cloned.1.call-start = ((), (), s32[]{:S(2)}) async-start(), calls=%async_computation.10 | async-start | bytes 15728640 | tf_op jit(solution)/shard_map/reduce_scatter | solution.py:56
  918.7 6.4 copy-start.25
  929.3 10.5 copy-start.29
  944.8 6.5 copy-start.9
  944.8 6.5 copy-start.11
  960.4 14.0 %copy-start.17 = (s32[1024,2]{0,1:T(2,128)}, s32[1024,2]{0,1:T(2,128)S(1)}, u32[]{:S(2)}) copy-start(s32[1024,2]{0,1:T(2,128)S(1)} %compare_select_fusion.4) | copy-start | bytes 24580
  974.3 100.0 %copy-start.19 = (f32[768]{0:T(1024)S(1)}, f32[768]{0:T(1024)}, u32[]{:S(2)}) copy-start(f32[768]{0:T(1024)} %get-tuple-element.4) | copy-start | bytes 9220
  1070.7 4.9 copy-start.6
  1226.0 84.6 %all-to-all-start.1 = ((bf16[1,4,1024,768]{3,1,0,2:T(4,128)(2,1)}), bf16[1,4,1024,768]{3,1,0,2:T(4,128)(2,1)}, u32[]{:S(2)}, u32[]{:S(2)}) async-start(bf16[1,4,1024,768]{3,1,0,2:T(4,128)(2,1)} %copy.99), calls=%async_computation.4 | async-start | bytes 12582912 | tf_op jit(solution)/shard_map/all_to_all | solution.py:110
  1233.9 4.9 copy-start.12
  1240.7 18.0 %copy-start.16 = (s32[16,64,2]{1,2,0:T(2,128)S(1)}, s32[16,64,2]{1,2,0:T(2,128)}, u32[]{:S(2)}) copy-start(s32[16,64,2]{1,2,0:T(2,128)} %param.31) | copy-start | bytes 24580
  1240.7 18.2 %copy-start.14 = (s32[1024,2]{0,1:T(2,128)S(1)}, s32[1024,2]{0,1:T(2,128)}, u32[]{:S(2)}) copy-start(s32[1024,2]{0,1:T(2,128)} %copy-done.13) | copy-start | bytes 24580
  1310.6 4.2 copy-start.18
  1314.9 15.3 %copy-start.4 = (bf16[16,64,768]{2,1,0:T(8,128)(2,1)S(1)}, bf16[16,64,768]{2,1,0:T(8,128)(2,1)}, u32[]{:S(2)}) copy-start(bf16[16,64,768]{2,1,0:T(8,128)(2,1)} %copy-done.3) | copy-start | bytes 4718596
  (6 other events, 7.1 us)
Sparse Core Ops, SparseCore 0:
  13.6 66.8 all-gather.3
  524.7 115.7 reduce-scatter.3
  645.7 62.8 all-gather.5
  738.4 112.6 reduce-scatter.5
  855.8 62.8 all-gather.7
  957.9 112.6 reduce-scatter.7
where the time goes:
time: 1350 us; the launch traced here: 1340 us
  local copies, waits for them, and re-layouts  514 us (38%)
  waiting for transfers between devices  501 us (37%)
  matrix products  177 us (13%)
  blocking collectives  82.4 us (6%)
  other arithmetic  40.9 us (3%)
  between operations  15.2 us (1%)
    gather x4, local copies, waits for them, and re-layouts, causal_bias(): bias_full = jnp.take(bias_rows, bucket_of(jnp.maximum(rel_pos, 0)), axis=1)  469 us
    reduce_scatter x2, waiting for transfers between devices, attention_block(): reduced = lax.psum_scatter(part_sum, 'tp', scatter_dimension=1, tiled=True)  211 us
    reduce_scatter x1, waiting for transfers between devices, ffn_block(): reduced = lax.psum_scatter(part_sum, 'tp', scatter_dimension=1, tiled=True)  113 us
    all_to_all x1, blocking collectives, moe_block(): received = lax.all_to_all(dispatched, ('tp', 'ep'), 0, 2, tiled=True)  82.4 us
    all_gather x1, waiting for transfers between devices, ffn_block(): gathered = lax.all_gather(normed, 'tp', axis=1, tiled=True)  62.9 us
    all_gather x2, waiting for transfers between devices, attention_block(): gathered = lax.all_gather(normed, 'tp', axis=1, tiled=True)  62.5 us
    all_to_all x1, waiting for transfers between devices, moe_block(): returned = lax.all_to_all(expert_result, ('tp', 'ep'), 2, 0, tiled=True)  51.6 us
    dot_general x1, matrix products, moe_block(): jnp.einsum('erf,efd->erd', expert_hidden, expert_out, preferred_element_t...  46.5 us
  transfers between devices with their start and end apart: 7, of which 6 were waited for; matrix products, arithmetic and copies ran while one was open for 38% of the time, Pallas kernels for 0%

commit v1 on v0

v1 whole, which is shorter than its diff:
```python
import functools

import jax
import jax.numpy as jnp
from jax import lax
from jax.experimental import pallas as pl
from jax.experimental.pallas import tpu as pltpu
from jax.sharding import PartitionSpec as P

EXACT_BUCKETS = 16
THRESHOLDS = (18, 20, 23, 26, 30, 34, 39, 45, 51, 58, 66, 76, 86, 98, 112)
EPSILON = 1e-6
GROUP = ('tp', 'ep')
MESH = pl.DeviceIdType.MESH


def rms_norm(rows_in, ln_scale):
    wide_rows = rows_in.astype(jnp.float32)
    inv_rms = lax.rsqrt(jnp.mean(wide_rows * wide_rows, axis=-1, keepdims=True) + EPSILON)
    return (wide_rows * inv_rms * ln_scale).astype(jnp.bfloat16)


def tp_exchange_permutes(blocks, tp):
    me = lax.axis_index('tp')
    out = lax.dynamic_update_index_in_dim(jnp.zeros_like(blocks), lax.dynamic_index_in_dim(blocks, me, 0), me, 0)
    for step in range(1, tp):
        block = lax.dynamic_index_in_dim(blocks, (me + step) % tp, 0)
        got = lax.ppermute(block, 'tp', [(i, (i + step) % tp) for i in range(tp)])
        out = lax.dynamic_update_index_in_dim(out, got, (me + tp - step) % tp, 0)
    return out


def gather_kernel(tp, ep, num_blocks, direct, hidden_ref, table_ref, *refs):
    sources, refs = refs[:num_blocks], refs[num_blocks:]
    seqs_ref, relay_ref, tables_ref, refs = refs[0], refs[1], refs[2], refs[3:]
    gathered, refs = refs[:num_blocks], refs[num_blocks:]
    stage_ref, stage_hidden_ref, send_sem, recv_sem, in_sem, out_sem = refs
    me_tp, me_ep = lax.axis_index('tp'), lax.axis_index('ep')
    right, left, across = lax.rem(me_tp + 1, tp), lax.rem(me_tp + tp - 1, tp), lax.rem(me_tp + 2, tp)
    east, west, beyond = lax.rem(me_ep + 2, ep), lax.rem(me_ep + ep - 2, ep), lax.rem(me_ep + 4, ep)
    partner = me_ep + 1 - 2 * lax.rem(me_ep, 2)
    peers = ({'tp': right}, {'tp': left}, {'tp': across}, {'ep': east}, {'ep': west}, {'ep': partner})
    to_right, to_left, to_across, to_east, to_west, to_partner = peers

    barrier = pltpu.get_barrier_semaphore()
    for peer in peers:
        pl.semaphore_signal(barrier, inc=1, device_id=peer, device_id_type=MESH)
    pl.semaphore_wait(barrier, len(peers))

    copies = []

    def send(source, target, peer):
        index = len(copies)
        copy = pltpu.make_async_remote_copy(src_ref=source, dst_ref=target, send_sem=send_sem.at[index], recv_sem=recv_sem.at[index],
                                            device_id=peer, device_id_type=MESH)
        copy.start()
        copies.append(copy)
        return copy

    rows = sources[0].shape[1]
    halves = (slice(0, rows // 2), slice(rows // 2, rows))
    sliced = [block for block in range(num_blocks) if block != direct]
    locals_in = [pltpu.make_async_copy(sources[block], stage_ref.at[block], in_sem.at[block]) for block in range(num_blocks)]
    locals_in.append(pltpu.make_async_copy(hidden_ref.at[me_tp], stage_hidden_ref, in_sem.at[num_blocks]))

    first = {}
    for block in sliced:
        first[block] = [send(sources[block].at[me_ep], gathered[block].at[me_tp, me_ep], peer) for peer in (to_right, to_left)]
    tables = [send(table_ref, tables_ref.at[me_tp], peer) for peer in (to_right, to_left, to_across)]
    for copy in locals_in:
        copy.start()
    tables_ref[me_tp] = table_ref[...]
    part = hidden_ref.shape[1] // 2
    relays = [send(hidden_ref.at[across, 0:part], relay_ref.at[0], to_right), send(hidden_ref.at[across, part:2 * part], relay_ref.at[1], to_left)]

    def share(block, group, index, span=None):
        ref = gathered[block]
        return ref.at[group, index] if span is None else ref.at[group, index, span]

    received = []
    forward, sideways = {}, {}
    for block in sliced:
        first[block][0].wait_recv()
        forward[block] = [send(share(block, left, me_ep, halves[0]), share(block, left, me_ep, halves[0]), to_right)]
        sideways[block] = {}
        for group, name in ((left, 'left'), (right, 'right')):
            if name == 'right':
                first[block][1].wait_recv()
                forward[block].append(send(share(block, right, me_ep, halves[1]), share(block, right, me_ep, halves[1]), to_left))
            whole = share(block, group, me_ep)
            sideways[block][name] = [send(whole, whole, to_east), send(whole, whole, to_west)]
            received.append(send(whole, whole, to_partner))
    core_half = ep // 2
    base = lax.rem(me_ep, 2) * core_half
    near = pl.ds(base, core_half)
    direct_first = [send(sources[direct].at[near], gathered[direct].at[me_tp, near], peer) for peer in (to_right, to_left)]
    swaps = [send(hidden_ref.at[right], seqs_ref.at[:, me_tp], to_right), send(hidden_ref.at[left], seqs_ref.at[:, me_tp], to_left)]
    for block in sliced:
        for copy in forward[block]:
            copy.wait_recv()
        whole = share(block, across, me_ep)
        sideways[block]['across'] = [send(whole, whole, to_east), send(whole, whole, to_west)]
        received.append(send(whole, whole, to_partner))
    for copy in relays:
        copy.wait_recv()
    swaps.append(send(relay_ref.at[0], seqs_ref.at[0:part, left], to_right))
    swaps.append(send(relay_ref.at[1], seqs_ref.at[part:2 * part, right], to_left))
    for copy in locals_in:
        copy.wait()
    locals_out = [pltpu.make_async_copy(stage_ref.at[block], gathered[block].at[me_tp], out_sem.at[block]) for block in range(num_blocks)]
    locals_out.append(pltpu.make_async_copy(stage_hidden_ref, seqs_ref.at[:, me_tp], out_sem.at[num_blocks]))
    for copy in locals_out:
        copy.start()

    def direct_ring():
        for copy in direct_first:
            copy.wait_recv()
        lower, upper = pl.ds(base, core_half // 2), pl.ds(base + core_half // 2, core_half // 2)
        last = [send(gathered[direct].at[left, lower], gathered[direct].at[left, lower], to_right),
                send(gathered[direct].at[right, upper], gathered[direct].at[right, upper], to_left)]
        for group in (left, right):
            received.append(send(gathered[direct].at[group, near], gathered[direct].at[group, near], to_partner))
        return last

    direct_last = None
    final = []
    groups = {'left': left, 'right': right, 'across': across}
    for count, block in enumerate(sliced):
        for name in ('left', 'right', 'across'):
            group = groups[name]
            sideways[block][name][0].wait_recv()
            pair = [send(share(block, group, west, halves[0]), share(block, group, west, halves[0]), to_east)]
            whole = share(block, group, west)
            received.append(send(whole, whole, to_partner))
            sideways[block][name][1].wait_recv()
            pair.append(send(share(block, group, east, halves[1]), share(block, group, east, halves[1]), to_west))
            whole = share(block, group, east)
            received.append(send(whole, whole, to_partner))
            final.append((block, group, pair))
        if count == 1:
            direct_last = direct_ring()
    for block, group, pair in final:
        for copy in pair:
            copy.wait_recv()
        whole = share(block, group, beyond)
        received.append(send(whole, whole, to_partner))
    for copy in direct_last:
        copy.wait_recv()
    whole = gathered[direct].at[across, near]
    received.append(send(whole, whole, to_partner))
    for copy in tables + swaps + received:
        copy.wait_recv()
    for copy in copies:
        copy.wait_send()
    for copy in locals_out:
        copy.wait()


def gather_all(hidden_in, table, blocks, direct, tp, ep):
    num_blocks = len(blocks)
    batch, local_seq, d_model = hidden_in.shape
    seqs = batch // tp
    hidden_view = hidden_in.reshape(tp, seqs, local_seq, d_model)
    views = [block.reshape(ep, block.shape[0] // ep, block.shape[1]) for block in blocks]
    any_spec = pl.BlockSpec(memory_space=pl.ANY)
    vmem_spec = pl.BlockSpec(memory_space=pltpu.VMEM)
    copies = 28 * (num_blocks - 1) + 7 + 9
    results = pl.pallas_call(
        functools.partial(gather_kernel, tp, ep, num_blocks, direct),
        in_specs=[any_spec, vmem_spec] + [any_spec] * num_blocks,
        out_specs=[any_spec, any_spec, vmem_spec] + [any_spec] * num_blocks,
        out_shape=[jax.ShapeDtypeStruct((seqs, tp, local_seq, d_model), hidden_in.dtype),
                   jax.ShapeDtypeStruct((2, seqs // 2, local_seq, d_model), hidden_in.dtype),
                   jax.ShapeDtypeStruct((tp,) + table.shape, table.dtype)]
        + [jax.ShapeDtypeStruct((tp,) + view.shape, view.dtype) for view in views],
        scratch_shapes=[pltpu.VMEM((num_blocks,) + views[0].shape, views[0].dtype), pltpu.VMEM((seqs, local_seq, d_model), hidden_in.dtype),
                        pltpu.SemaphoreType.DMA((copies,)), pltpu.SemaphoreType.DMA((copies,)),
                        pltpu.SemaphoreType.DMA((num_blocks + 1,)), pltpu.SemaphoreType.DMA((num_blocks + 1,))],
        compiler_params=pltpu.CompilerParams(collective_id=0, has_side_effects=True),
        name='gather_all',
    )(hidden_view, table, *views)
    hidden = results[0].reshape(seqs, tp * local_seq, d_model)
    tables = jnp.swapaxes(results[2], 0, 1).reshape(table.shape[0], -1, table.shape[2])
    return hidden, tables, [block.reshape(tp, -1, d_model) for block in results[3:]]


def attention_kernel(tp, hidden_ref, ln_ref, w_ref, table_ref, out_ref, keys_ref, values_ref, bias_ref, q_ref, kt_ref, ctx_ref, w_out_ref):
    seq_len, d_model = hidden_ref.shape[1], hidden_ref.shape[2]
    num_heads = table_ref.shape[0]
    head_dim = d_model // num_heads
    half = seq_len // 2
    width = d_model // tp
    starts = tuple(range(EXACT_BUCKETS + 1)) + THRESHOLDS

    @pl.when(pl.program_id(0) == 0)
    def _():
        def one_head(head, carry):
            for block in range(2):
                key_pos = lax.broadcasted_iota(jnp.int32, (half, half), 0)
                query_pos = lax.broadcasted_iota(jnp.int32, (half, half), 1) + block * half
                rel_pos = query_pos - key_pos
                bias = jnp.full((half, half), -jnp.inf, jnp.float32)
                for bucket, start in enumerate(starts):
                    bias = jnp.where(rel_pos >= start, table_ref[head, bucket], bias)
                bias_ref[head, :, block * half:(block + 1) * half] = bias
            return carry

        lax.fori_loop(0, num_heads, one_head, 0)
        for part in range(tp):
            w_out_ref[part * width:(part + 1) * width] = w_ref[part, 3 * width:]

    rows = hidden_ref[0].astype(jnp.float32)
    inv_rms = lax.rsqrt(jnp.mean(rows * rows, axis=-1, keepdims=True) + EPSILON)
    normed = (rows * inv_rms * ln_ref[...]).astype(jnp.bfloat16)
    nt = (((1,), (1,)), ((), ()))
    for part in range(tp):
        take = slice(part * width, (part + 1) * width)
        qkv = lax.dot_general(w_ref[part, :3 * width], normed, nt, preferred_element_type=jnp.float32).astype(jnp.bfloat16)
        q_ref[take] = qkv[:width]
        keys_ref[part, 0] = qkv[width:2 * width]
        values_ref[part, 0] = qkv[2 * width:]
        kt_ref[take] = qkv[width:2 * width]

    local_heads = num_heads // tp
    zeros = jnp.zeros((head_dim, seq_len), jnp.bfloat16)
    for head in range(num_heads):
        pair = slice((head // 2) * 2 * head_dim, (head // 2 + 1) * 2 * head_dim)
        q_head = q_ref[head * head_dim:(head + 1) * head_dim]
        q_pair = jnp.concatenate([q_head, zeros] if head % 2 == 0 else [zeros, q_head], axis=0)
        scores = jnp.dot(kt_ref[pair].T, q_pair, preferred_element_type=jnp.float32)
        value = values_ref[head // local_heads, 0, (head % local_heads) * head_dim:(head % local_heads + 1) * head_dim]
        near, far = bias_ref[head, :, :half], bias_ref[head, :, half:]
        scale = head_dim ** -0.5
        first = scores[:half, :half] * scale + near
        first = jnp.exp(first - jnp.max(first, axis=0, keepdims=True))
        probs = (first / jnp.sum(first, axis=0, keepdims=True)).astype(jnp.bfloat16)
        ctx_first = jnp.dot(value[:, :half], probs, preferred_element_type=jnp.float32)
        low = scores[:half, half:] * scale + far
        high = scores[half:, half:] * scale + near
        top = jnp.maximum(jnp.max(low, axis=0, keepdims=True), jnp.max(high, axis=0, keepdims=True))
        low, high = jnp.exp(low - top), jnp.exp(high - top)
        total = jnp.sum(low, axis=0, keepdims=True) + jnp.sum(high, axis=0, keepdims=True)
        probs = jnp.concatenate([(low / total).astype(jnp.bfloat16), (high / total).astype(jnp.bfloat16)], axis=0)
        ctx_second = jnp.dot(value, probs, preferred_element_type=jnp.float32)
        ctx = jnp.concatenate([ctx_first, ctx_second], axis=1)
        ctx_ref[head * head_dim:(head + 1) * head_dim] = ctx.astype(jnp.bfloat16)
    attn_out = jnp.dot(ctx_ref[...].T, w_out_ref[...], preferred_element_type=jnp.float32)
    out_ref[0] = (rows + attn_out).astype(jnp.bfloat16)


def attention(hidden, ln_scale, packed, table, tp):
    seqs, seq_len, d_model = hidden.shape
    num_heads = table.shape[0]
    width = d_model // tp
    seq_block = pl.BlockSpec((1, seq_len, d_model), lambda s: (s, 0, 0))
    cache_block = pl.BlockSpec((tp, 1, width, seq_len), lambda s: (0, s, 0, 0))
    cache = jax.ShapeDtypeStruct((tp, seqs, width, seq_len), jnp.bfloat16)
    flops = 2 * seqs * seq_len * d_model * (5 * d_model + 3 * seq_len)
    return pl.pallas_call(
        functools.partial(attention_kernel, tp),
        grid=(seqs,),
        in_specs=[seq_block, pl.BlockSpec((1, d_model), lambda s: (0, 0)), pl.BlockSpec((tp, d_model, d_model), lambda s: (0, 0, 0)),
                  pl.BlockSpec(memory_space=pltpu.SMEM)],
        out_specs=[seq_block, cache_block, cache_block],
        out_shape=[jax.ShapeDtypeStruct(hidden.shape, hidden.dtype), cache, cache],
        scratch_shapes=[pltpu.VMEM((num_heads, seq_len // 2, seq_len), jnp.float32), pltpu.VMEM((d_model, seq_len), jnp.bfloat16),
                        pltpu.VMEM((d_model, seq_len), jnp.bfloat16), pltpu.VMEM((d_model, seq_len), jnp.bfloat16),
                        pltpu.VMEM((d_model, d_model), jnp.bfloat16)],
        compiler_params=pltpu.CompilerParams(dimension_semantics=('arbitrary',), vmem_limit_bytes=40 * 1024 * 1024),
        cost_estimate=pl.CostEstimate(flops=flops, bytes_accessed=2 * (hidden.size * 4 + packed.size), transcendentals=0),
        name='attention',
    )(hidden, ln_scale[None], packed, table)


def dense_ffn(hidden, ln_scale, gate, up, down):
    normed = rms_norm(hidden, ln_scale)
    gate_pre = jnp.einsum('std,gdf->stgf', normed, gate, preferred_element_type=jnp.float32)
    up_pre = jnp.einsum('std,gdf->stgf', normed, up, preferred_element_type=jnp.float32)
    ffn_hidden = (jax.nn.gelu(gate_pre) * up_pre).astype(jnp.bfloat16)
    ffn_out = jnp.einsum('stgf,gfd->std', ffn_hidden, down, preferred_element_type=jnp.float32)
    return (hidden.astype(jnp.float32) + ffn_out).astype(jnp.bfloat16)


def slot_table(choices, num_experts):
    experts = jnp.arange(num_experts, dtype=jnp.int32)
    first_hot = (choices[..., 0:1] == experts).astype(jnp.int32)
    second_hot = (choices[..., 1:2] == experts).astype(jnp.int32)
    first_pos = jnp.sum((jnp.cumsum(first_hot, axis=-2) - 1) * first_hot, axis=-1)
    second_base = jnp.cumsum(second_hot, axis=-2) - 1 + jnp.sum(first_hot, axis=-2, keepdims=True)
    second_pos = jnp.sum(second_base * second_hot, axis=-1)
    return jnp.stack([first_pos, second_pos], axis=-1)


def moe_block(hidden, ln_scale, w_router, expert_in, expert_out, expert_ids, caches):
    local_batch, local_seq, d_model = hidden.shape
    tokens = local_batch * local_seq
    num_experts = w_router.shape[1]
    local_experts = expert_in.shape[0]
    groups = num_experts // local_experts
    capacity = 4 * tokens // num_experts
    choices = expert_ids.reshape(tokens, 2)
    position = slot_table(choices, num_experts)
    slot_ids = jnp.where(position < capacity, choices * capacity + position, -1)
    columns = jnp.arange(num_experts * capacity, dtype=jnp.int32)
    select = (slot_ids[:, :, None] == columns).astype(jnp.bfloat16)

    normed = rms_norm(hidden, ln_scale).reshape(tokens, d_model)
    dispatched = jnp.einsum('ncs,nd->sd', select, normed, preferred_element_type=jnp.float32).astype(jnp.bfloat16)
    dispatched = dispatched.reshape(groups, local_experts, capacity, d_model)
    received = lax.all_to_all(dispatched, GROUP, 0, 2, tiled=True)
    expert_rows = received.reshape(local_experts, groups * capacity, d_model)

    logits = jnp.dot(normed.astype(jnp.float32), w_router, precision=lax.Precision.HIGHEST)
    router_probs = jax.nn.softmax(logits, axis=-1)
    experts = jnp.arange(num_experts, dtype=jnp.int32)
    picked = jnp.sum(jnp.where(choices[:, :, None] == experts, router_probs[:, None, :], 0.0), axis=-1)
    gate_weights = picked / jnp.sum(picked, axis=-1, keepdims=True)

    expert_hidden = jnp.einsum('erd,edf->erf', expert_rows, expert_in, preferred_element_type=jnp.float32)
    expert_hidden = jax.nn.gelu(expert_hidden).astype(jnp.bfloat16)
    expert_result = jnp.einsum('erf,efd->erd', expert_hidden, expert_out, preferred_element_type=jnp.float32).astype(jnp.bfloat16)
    expert_result, *caches = lax.optimization_barrier((expert_result, *caches))
    expert_result = expert_result.reshape(1, local_experts, groups * capacity, d_model)
    returned = lax.all_to_all(expert_result, GROUP, 2, 0, tiled=True)
    returned = returned.reshape(num_experts * capacity, d_model)
    gathered_out = jnp.einsum('ncs,sd->ncd', select, returned, preferred_element_type=jnp.float32)
    moe_sum = jnp.sum(gate_weights[:, :, None] * gathered_out, axis=1).reshape(local_batch, local_seq, d_model)
    return (hidden.astype(jnp.float32) + moe_sum).astype(jnp.bfloat16), *caches


def solution(mesh):
    tp, ep = mesh.shape['tp'], mesh.shape['ep']
    act_spec = P(('dp', 'ep'), 'tp', None)
    col_spec = P(None, None, 'tp')
    row_spec = P(None, 'tp', None)
    expert_spec = P(('tp', 'ep'), None, None)
    cache_spec = P(None, ('dp', 'ep'), 'tp', None, None)
    in_specs = (act_spec, P(), P(), col_spec, col_spec, col_spec, row_spec, row_spec,
                P(None, 'tp'), P(None, 'tp'), P('tp', None), P(), expert_spec, expert_spec, act_spec)

    def to_owner(blocks, local_heads):
        got = tp_exchange_permutes(blocks, tp)
        return jnp.swapaxes(got.reshape(got.shape[0] * got.shape[1], local_heads, -1, got.shape[3]), 2, 3)

    def device_fn(hidden_in, ln_attn, ln_ffn, w_query, w_key, w_value, w_out, bias_table, w_gate, w_up, w_down, w_router, expert_in, expert_out, expert_ids):
        def packed(layer):
            parts = [jnp.swapaxes(w[layer], 0, 1) for w in (w_query, w_key, w_value)] + [w_out[layer]]
            return jnp.concatenate(parts, axis=0)

        local_heads = bias_table.shape[1]
        blocks = [packed(0), w_up, w_down, packed(1), w_gate]
        hidden, tables, (attn_zero, up, down, attn_one, gate) = gather_all(hidden_in, bias_table, blocks, len(blocks) - 1, tp, ep)
        hidden, keys_zero, values_zero = attention(hidden, ln_attn[0], attn_zero, tables[0], tp)
        keys_zero, values_zero = to_owner(keys_zero, local_heads), to_owner(values_zero, local_heads)
        hidden = dense_ffn(hidden, ln_ffn[0], gate, up, down)
        hidden, keys_one, values_one = attention(hidden, ln_attn[1], attn_one, tables[1], tp)
        hidden, keys_zero, values_zero = lax.optimization_barrier((hidden, keys_zero, values_zero))
        keys_one, values_one = to_owner(keys_one, local_heads), to_owner(values_one, local_heads)
        hidden = lax.all_to_all(hidden, 'tp', 1, 0, tiled=True)
        hidden, keys_one, values_one = moe_block(hidden, ln_ffn[1], w_router, expert_in, expert_out, expert_ids, (keys_one, values_one))
        keys, values = jnp.stack([keys_zero, keys_one]), jnp.stack([values_zero, values_one])
        return hidden, keys, values

    return jax.shard_map(device_fn, mesh=mesh, in_specs=in_specs, out_specs=(act_spec, cache_spec, cache_spec), check_vma=False)
```

time: 1350 us -> 530 us (0.39)
  the two profiles are of different devices: /device:TPU:97 before, /device:TPU:103 now
where the time goes in v1:
time: 530 us; the launch traced here: 523 us
  waiting for transfers between devices  169 us (32%)
  Pallas kernels  121 us (23%)
  matrix products  105 us (20%)
  local copies, waits for them, and re-layouts  58 us (11%)
  starting transfers between devices  36 us (7%)
  other arithmetic  32.7 us (6%)
    ppermute x12, waiting for transfers between devices, tp_exchange_permutes(): got = lax.ppermute(block, 'tp', [(i, (i + step) % tp) for i in range(tp)])  95.1 us
    pallas_call x1, Pallas kernels, gather_all(): pl.pallas_call(functools.partial(gather_kernel, tp, ep, num_blocks, direc...  74.6 us
    all_to_all x1, waiting for transfers between devices, moe_block(): returned = lax.all_to_all(expert_result, GROUP, 2, 0, tiled=True)  72.1 us
    dot_general x1, matrix products, moe_block(): jnp.einsum('erf,efd->erd', expert_hidden, expert_out, preferred_element_t...  46.5 us
    pallas_call x2, Pallas kernels, attention(): pl.pallas_call(functools.partial(attention_kernel, tp), grid=(seqs,), in_...  46.2 us
    dot_general x1, matrix products, dense_ffn(): jnp.einsum('stgf,gfd->std', ffn_hidden, down, preferred_element_type=jnp....  18.7 us
    ppermute x12, starting transfers between devices, tp_exchange_permutes(): got = lax.ppermute(block, 'tp', [(i, (i + step) % tp) for i in range(tp)])  16.6 us
    dot_general x1, matrix products, moe_block(): jnp.einsum('ncs,sd->ncd', select, returned, preferred_element_type=jnp.fl...  15 us
  transfers between devices with their start and end apart: 15, of which 6 were waited for; matrix products, arithmetic and copies ran while one was open for 14% of the time, Pallas kernels for 4%

profile of v1, /device:TPU:103, one launch (start us, length us, event | category | flops | bytes accessed | tf_op | source)
XLA Modules:
  0.0 523.1 jit_solution(16912139799941216184)
XLA Ops:
  6.3 74.6 %gather_all.1 = (bf16[4,4,64,768]{3,2,1,0:T(8,128)(2,1)}, bf16[2,2,64,768]{3,2,1,0:T(8,128)(2,1)}, f32[4,2,3,32]{3,2,1,0:T(4,128)}, bf16[4,8,96,768]{3,2,1,0:T(8...) custom-call(bf16[4,4,64,768]{3,2,1,0:T(8,128)(2,1)} %bitcast.159, ...), custom_call_target="tpu_custom_call" | custom-call | tf_op jit(solution)/shard_map/gather_all/pallas_call | solution.py:168
  81.6 2.3 copy-done.4
  85.4 22.9 %attention.2 = (bf16[4,256,768]{2,1,0:T(8,128)(2,1)S(1)}, bf16[4,4,192,256]{3,2,1,0:T(8,128)(2,1)S(1)}, bf16[4,4,192,256]{3,2,1,0:T(8,128)(2,1)S(1)}) custom-call(bf16[4,256,768]{2,1,0:T(8,128)(2,1)S(1)} %bitcast.145, f32[1,768]{1,0:T(1,128)S(1)} %get-tuple-element.76.ln_ref, bf16[4,768,768]{2,1,0:T(8,128)(2,1)S(1)} %bitcast.144, f32[12,32]{1,0:T(8,128)S(1)} %squeeze.38.table_ref), custom_call_target="tpu_custom_call" | custom-call | flops 7247757312 | bytes 11010048 | tf_op jit(solution)/shard_map/attention/pallas_call | solution.py:259
  114.2 1.9 collective-permute-start.1
  119.7 10.3 %fusion.42 = f32[4,256,4,768]{3,1,2,0:T(8,128)} fusion(bf16[4,768,768,1]{2,1,0,3:T(8,128)(2,1)} %bitcast.173, bf16[4,256,768]{2,1,0:T(8,128)(2,1)S(1)} %get-tuple-element.25, f32[768]{0:T(1024)S(1)} %get-tuple-element.44, f32[4,256]{1,0:T(4,128)S(1)} %add_rsqrt_fusion.1), kind=kOutput, calls=%fused_computation.50 | convolution fusion | flops 4834983936 | bytes 18881536 | tf_op jit(solution)/shard_map/std,gdf->stgf/dot_general | solution.py:277
  130.1 18.7 %fusion.31.hidden_ref = bf16[4,256,768]{2,1,0:T(8,128)(2,1)} fusion(bf16[4,256,768]{2,1,0:T(8,128)(2,1)S(1)} %get-tuple-element.25, bf16[4,768,768,1]{2,1,0,3:T(8,128)(2,1)} %bitcast.172, f32[4,256,4,768]{3,1,2,0:T(8,128)} %fusion.42, bf16[4,768,768,1]{2,1,0,3:T(8,128)(2,1)} %bitcast.171, f32[768]{0:T(1024)S(1)} %get-tuple-element.44, ...), kind=kOutput, calls=%fused_computation.39 | convolution fusion | flops 9700638720 | bytes 25172992 | tf_op jit(solution)/shard_map/stgf,gfd->std/dot_general | solution.py:280
  148.8 2.3 copy-done.3
  152.5 23.3 %attention.3 = (bf16[4,256,768]{2,1,0:T(8,128)(2,1)S(1)}, bf16[4,4,192,256]{3,2,1,0:T(8,128)(2,1)S(1)}, bf16[4,4,192,256]{3,2,1,0:T(8,128)(2,1)S(1)}) custom-call(bf16[4,256,768]{2,1,0:T(8,128)(2,1)S(1)} %copy-done.6, f32[1,768]{1,0:T(1,128)S(1)} %get-tuple-element.75.ln_ref, bf16[4,768,768]{2,1,0:T(8,128)(2,1)S(1)} %bitcast.143, f32[12,32]{1,0:T(8,128)S(1)} %squeeze.39.table_ref), custom_call_target="tpu_custom_call" | custom-call | flops 7247757312 | bytes 11010048 | tf_op jit(solution)/shard_map/attention/pallas_call | solution.py:259
  179.5 1.9 collective-permute-start.2
  191.1 2.4 copy.92
  193.5 3.8 all-to-all-start
  200.3 13.8 %convert_reduce_fusion = bf16[1024,4096]{1,0:T(8,128)(2,1)} fusion(s32[1024,2]{0,1:T(2,128)S(1)} %compare_select_fusion), kind=kLoop, calls=%fused_computation.9 | loop fusion | flops 29360128 | bytes 8396800 | tf_op jit(solution)/shard_map/ncs,nd->sd/reduce_sum | solution.py:308
  216.2 2.0 copy.94
  218.7 2.2 fusion.33
  221.0 13.0 %fusion.72 = bf16[4096,768]{1,0:T(8,128)(2,1)} fusion(bf16[1024,4096]{1,0:T(8,128)(2,1)} %convert_reduce_fusion, bf16[1024,768]{1,0:T(8,128)(2,1)S(1)} %fusion.33), kind=kOutput, calls=%fused_computation.138 | convolution fusion | flops 6442450944 | bytes 16252928 | tf_op jit(solution)/shard_map/ncs,nd->sd/dot_general | solution.py:308
  234.0 7.3 %all-to-all-start.1 = ((bf16[32,4,32,768]{3,2,1,0:T(8,128)(2,1)}), bf16[32,4,32,768]{3,2,1,0:T(8,128)(2,1)}, u32[]{:S(2)}, u32[]{:S(2)}) async-start(bf16[32,4,32,768]{3,2,1,0:T(8,128)(2,1)} %bitcast.147), calls=%async_computation.1 | async-start | bytes 12582912 | tf_op jit(solution)/shard_map/all_to_all | solution.py:310
  243.0 2.8 collective-permute-start.10
  248.4 65.7 %collective-permute-done.9 = bf16[1,4,192,256]{3,2,1,0:T(8,128)(2,1)S(1)} collective-permute-done((bf16[1,4,192,256]{3,2,1,0:T(8,128)(2,1)S(1)}, bf16[1,4,192,256]{3,2,1,0:T(8,128)(2,1)S(1)}, u32[]{:S(2)}, u32[]{:S(2)}) %collective-permute-start.9) | collective-permute-done | bytes 393248 | tf_op jit(solution)/shard_map/ppermute | solution.py:28
  314.1 2.8 collective-permute-start.8
  317.0 12.7 %collective-permute-done.10 = bf16[1,4,192,256]{3,2,1,0:T(8,128)(2,1)S(1)} collective-permute-done((bf16[1,4,192,256]{3,2,1,0:T(8,128)(2,1)S(1)}, bf16[1,4,192,256]{3,2,1,0:T(8,128)(2,1)S(1)}, u32[]{:S(2)}, u32[]{:S(2)}) %collective-permute-start.10) | collective-permute-done | bytes 393248 | tf_op jit(solution)/shard_map/ppermute | solution.py:28
  329.7 3.8 collective-permute-done.6
  333.5 13.0 %collective-permute-done.7 = bf16[1,4,192,256]{3,2,1,0:T(8,128)(2,1)S(1)} collective-permute-done((bf16[1,4,192,256]{3,2,1,0:T(8,128)(2,1)S(1)}, bf16[1,4,192,256]{3,2,1,0:T(8,128)(2,1)S(1)}, u32[]{:S(2)}, u32[]{:S(2)}) %collective-permute-start.7) | collective-permute-done | bytes 393248 | tf_op jit(solution)/shard_map/ppermute | solution.py:28
  346.6 6.1 %copy.103 = bf16[1,4,32,32,768]{4,3,2,1,0:T(8,128)(2,1)} copy(bf16[1,4,32,32,768]{4,3,1,2,0:T(8,128)(2,1)} %bitcast.59) | data formatting | bytes 12582912 | tf_op jit(solution)/shard_map/all_to_all | solution.py:310
  352.7 46.5 %fusion.27 = bf16[4,1024,768]{2,1,0:T(8,128)(2,1)} fusion(bf16[4,3072,768]{2,1,0:T(8,128)(2,1)} %param.28, bf16[4,1024,768]{2,1,0:T(8,128)(2,1)} %bitcast.149, bf16[4,768,3072]{2,1,0:T(8,128)(2,1)} %param.27), kind=kOutput, calls=%fused_computation.35 | convolution fusion | flops 38771097600 | bytes 50331648 | tf_op jit(solution)/shard_map/erf,efd->erd/dot_general | solution.py:321
  399.2 10.3 %copy.104 = bf16[1,4,1024,768]{3,1,0,2:T(4,128)(2,1)} copy(bf16[1,4,1024,768]{3,2,1,0:T(8,128)(2,1)} %bitcast.150) | data formatting | bytes 12582912 | tf_op jit(solution)/shard_map/reshape | solution.py:323
  409.5 8.4 %all-to-all-start.2 = ((bf16[1,4,1024,768]{3,1,0,2:T(4,128)(2,1)}), bf16[1,4,1024,768]{3,1,0,2:T(4,128)(2,1)}, u32[]{:S(2)}, u32[]{:S(2)}) async-start(bf16[1,4,1024,768]{3,1,0,2:T(4,128)(2,1)} %copy.104), calls=%async_computation.2 | async-start | bytes 12582912 | tf_op jit(solution)/shard_map/all_to_all | solution.py:324
  420.6 2.0 copy.98
  424.5 3.5 pad_maximum_fusion.1
  428.0 1.9 pad_maximum_fusion
  429.9 72.1 %all-to-all-done.2 = bf16[1,4,1024,768]{3,1,0,2:T(4,128)(2,1)} async-done(((bf16[1,4,1024,768]{3,1,0,2:T(4,128)(2,1)}), bf16[1,4,1024,768]{3,1,0,2:T(4,128)(2,1)}, u32[]{:S(2)}, u32[]{:S(2)}) %all-to-all-start.2) | async-done | bytes 6291488 | tf_op jit(solution)/shard_map/all_to_all | solution.py:324
  502.0 4.2 copy.105
  506.2 15.0 %multiply_reduce_fusion = f32[1024,768]{1,0:T(8,128)S(1)} fusion(f32[1024,2]{0,1:T(2,128)S(1)} %broadcast_divide_fusion, bf16[4096,768,1]{1,0,2:T(8,128)(2,1)S(1)} %bitcast.148, s32[1024,2]{0,1:T(2,128)S(1)} %copy-done.25), kind=kOutput, calls=%fused_computation.30 | convolution fusion | flops 12895649792 | bytes 9453568 | tf_op jit(solution)/shard_map/ncs,sd->ncd/dot_general | solution.py:326
  (143 shorter events, 48.2 us)
Async XLA Ops:
  0.6 417.3 %copy-start = (f32[768,128]{1,0:T(8,128)S(1)}, f32[768,128]{1,0:T(8,128)}, u32[]{:S(2)}) copy-start(f32[768,128]{1,0:T(8,128)} %param.26) | copy-start | bytes 1179652
  6.3 75.3 %copy-start.29 = (f32[2,768]{1,0:T(2,128)S(1)}, f32[2,768]{1,0:T(2,128)}, u32[]{:S(2)}) copy-start(f32[2,768]{1,0:T(2,128)} %param.16) | copy-start | bytes 18436
  109.5 6.9 %copy-start.10 = (bf16[4,4,192,256]{3,2,1,0:T(8,128)(2,1)}, bf16[4,4,192,256]{3,2,1,0:T(8,128)(2,1)S(1)}, u32[]{:S(2)}) copy-start(bf16[4,4,192,256]{3,2,1,0:T(8,128)(2,1)S(1)} %get-tuple-element.58) | copy-start | bytes 4718596
  109.5 70.0 %collective-permute-start.3 = (bf16[1,4,192,256]{3,2,1,0:T(8,128)(2,1)}, bf16[1,4,192,256]{3,2,1,0:T(8,128)(2,1)}, u32[]{:S(2)}, u32[]{:S(2)}) collective-permute-start(bf16[1,4,192,256]{3,2,1,0:T(8,128)(2,1)} %get-tuple-element.57), channel_id=1, source_target_pairs={{0,8},{8,16},{16,24},{24,0},{1,9},{9,17},{17,25},{25,1},{2,10},{10... | collective-permute-start | bytes 1179656 | tf_op jit(solution)/shard_map/ppermute | solution.py:28
  109.5 73.7 %collective-permute-start.4 = (bf16[1,4,192,256]{3,2,1,0:T(8,128)(2,1)}, bf16[1,4,192,256]{3,2,1,0:T(8,128)(2,1)}, u32[]{:S(2)}, u32[]{:S(2)}) collective-permute-start(bf16[1,4,192,256]{3,2,1,0:T(8,128)(2,1)} %get-tuple-element.56), channel_id=1, source_target_pairs={{0,16},{8,24},{16,0},{24,8},{1,17},{9,25},{17,1},{25,9},{2,18},{10... | collective-permute-start | bytes 1179656 | tf_op jit(solution)/shard_map/ppermute | solution.py:28
  110.6 74.4 %collective-permute-start.5 = (bf16[1,4,192,256]{3,2,1,0:T(8,128)(2,1)}, bf16[1,4,192,256]{3,2,1,0:T(8,128)(2,1)}, u32[]{:S(2)}, u32[]{:S(2)}) collective-permute-start(bf16[1,4,192,256]{3,2,1,0:T(8,128)(2,1)} %get-tuple-element.55), channel_id=1, source_target_pairs={{0,24},{8,0},{16,8},{24,16},{1,25},{9,1},{17,9},{25,17},{2,26},{10... | collective-permute-start | bytes 1179656 | tf_op jit(solution)/shard_map/ppermute | solution.py:28
  112.2 4.3 copy-start.28
  112.2 4.9 copy-start.27
  113.4 73.4 %collective-permute-start = (bf16[1,4,192,256]{3,2,1,0:T(8,128)(2,1)}, bf16[1,4,192,256]{3,2,1,0:T(8,128)(2,1)}, u32[]{:S(2)}, u32[]{:S(2)}) collective-permute-start(bf16[1,4,192,256]{3,2,1,0:T(8,128)(2,1)} %get-tuple-element.61), channel_id=1, source_target_pairs={{0,8},{8,16},{16,24},{24,0},{1,9},{9,17},{17,25},{25,1},{2,10},{10... | collective-permute-start | bytes 1179656 | tf_op jit(solution)/shard_map/ppermute | solution.py:28
  114.2 74.4 %collective-permute-start.1 = (bf16[1,4,192,256]{3,2,1,0:T(8,128)(2,1)}, bf16[1,4,192,256]{3,2,1,0:T(8,128)(2,1)}, u32[]{:S(2)}, u32[]{:S(2)}) collective-permute-start(bf16[1,4,192,256]{3,2,1,0:T(8,128)(2,1)} %get-tuple-element.60), channel_id=1, source_target_pairs={{0,16},{8,24},{16,0},{24,8},{1,17},{9,25},{17,1},{25,9},{2,18},{10... | collective-permute-start | bytes 1179656 | tf_op jit(solution)/shard_map/ppermute | solution.py:28
  152.5 24.5 %copy-start.18 = (s32[8,128]{0,1:T(8,128)S(1)}, s32[8,128]{0,1:T(8,128)}, u32[]{:S(2)}) copy-start(s32[8,128]{0,1:T(8,128)} %copy.101) | copy-start | bytes 12292
  152.5 25.5 %copy-start.16 = (s32[128,8,128]{0,1,2:T(8,128)S(1)}, s32[128,8,128]{0,1,2:T(8,128)}, u32[]{:S(2)}) copy-start(s32[128,8,128]{0,1,2:T(8,128)} %add_add_fusion.1) | copy-start | bytes 1572868
  179.5 10.8 %collective-permute-start.2 = (bf16[1,4,192,256]{3,2,1,0:T(8,128)(2,1)}, bf16[1,4,192,256]{3,2,1,0:T(8,128)(2,1)S(1)}, u32[]{:S(2)}, u32[]{:S(2)}) collective-permute-start(bf16[1,4,192,256]{3,2,1,0:T(8,128)(2,1)} %get-tuple-element.59), channel_id=1, source_target_pairs={{0,24},{8,0},{16,8},{24,16},{1,25},{9,1},{17,9},{25,17},{2,26},{10... | collective-permute-start | bytes 1179656 | tf_op jit(solution)/shard_map/ppermute | solution.py:28
  193.5 5.0 copy-start.23
  193.5 6.8 %copy-start.20 = (s32[1024,2]{0,1:T(2,128)S(1)}, s32[1024,2]{0,1:T(2,128)}, u32[]{:S(2)}) copy-start(s32[1024,2]{0,1:T(2,128)} %copy-done.19) | copy-start | bytes 24580
  193.5 22.4 %all-to-all-start = ((bf16[4,256,768]{2,0,1:T(4,128)(2,1)}), bf16[4,256,768]{2,0,1:T(4,128)(2,1)S(1)}, u32[]{:S(2)}, u32[]{:S(2)}) async-start(bf16[4,256,768]{2,0,1:T(4,128)(2,1)} %copy.92), calls=%async_computation | async-start | bytes 3145728 | tf_op jit(solution)/shard_map/all_to_all | solution.py:359
  200.3 13.8 %copy-start.24 = (s32[1024,2]{0,1:T(2,128)}, s32[1024,2]{0,1:T(2,128)S(1)}, u32[]{:S(2)}) copy-start(s32[1024,2]{0,1:T(2,128)S(1)} %compare_select_fusion) | copy-start | bytes 24580
  221.0 13.0 %copy-start.8 = (bf16[1024,768]{1,0:T(8,128)(2,1)}, bf16[1024,768]{1,0:T(8,128)(2,1)S(1)}, u32[]{:S(2)}) copy-start(bf16[1024,768]{1,0:T(8,128)(2,1)S(1)} %fusion.33) | copy-start | bytes 4718596
  234.0 7.4 %copy-start.2 = (bf16[4,4,192,256]{3,2,1,0:T(8,128)(2,1)S(1)}, bf16[4,4,192,256]{3,2,1,0:T(8,128)(2,1)}, u32[]{:S(2)}) copy-start(bf16[4,4,192,256]{3,2,1,0:T(8,128)(2,1)} %copy-done.1) | copy-start | bytes 4718596
  234.0 112.6 %all-to-all-start.1 = ((bf16[32,4,32,768]{3,2,1,0:T(8,128)(2,1)}), bf16[32,4,32,768]{3,2,1,0:T(8,128)(2,1)}, u32[]{:S(2)}, u32[]{:S(2)}) async-start(bf16[32,4,32,768]{3,2,1,0:T(8,128)(2,1)} %bitcast.147), calls=%async_computation.1 | async-start | bytes 12582912 | tf_op jit(solution)/shard_map/all_to_all | solution.py:310
  241.6 72.5 %collective-permute-start.9 = (bf16[1,4,192,256]{3,2,1,0:T(8,128)(2,1)S(1)}, bf16[1,4,192,256]{3,2,1,0:T(8,128)(2,1)S(1)}, u32[]{:S(2)}, u32[]{:S(2)}) collective-permute-start(bf16[1,4,192,256]{3,2,1,0:T(8,128)(2,1)S(1)} %get-tuple-element.49), channel_id=1, source_target_pairs={{0,8},{8,16},{16,24},{24,0},{1,9},{9,17},{17,25},{25,1},{2,10},{10... | collective-permute-start | bytes 1179656 | tf_op jit(solution)/shard_map/ppermute | solution.py:28
  243.0 86.6 %collective-permute-start.10 = (bf16[1,4,192,256]{3,2,1,0:T(8,128)(2,1)S(1)}, bf16[1,4,192,256]{3,2,1,0:T(8,128)(2,1)S(1)}, u32[]{:S(2)}, u32[]{:S(2)}) collective-permute-start(bf16[1,4,192,256]{3,2,1,0:T(8,128)(2,1)S(1)} %get-tuple-element.48), channel_id=1, source_target_pairs={{0,16},{8,24},{16,0},{24,8},{1,17},{9,25},{17,1},{25,9},{2,18},{10... | collective-permute-start | bytes 1179656 | tf_op jit(solution)/shard_map/ppermute | solution.py:28
  245.8 83.8 %collective-permute-start.11 = (bf16[1,4,192,256]{3,2,1,0:T(8,128)(2,1)S(1)}, bf16[1,4,192,256]{3,2,1,0:T(8,128)(2,1)S(1)}, u32[]{:S(2)}, u32[]{:S(2)}) collective-permute-start(bf16[1,4,192,256]{3,2,1,0:T(8,128)(2,1)S(1)} %get-tuple-element.47), channel_id=1, source_target_pairs={{0,24},{8,0},{16,8},{24,16},{1,25},{9,1},{17,9},{25,17},{2,26},{10... | collective-permute-start | bytes 1179656 | tf_op jit(solution)/shard_map/ppermute | solution.py:28
  247.1 86.4 %collective-permute-start.6 = (bf16[1,4,192,256]{3,2,1,0:T(8,128)(2,1)S(1)}, bf16[1,4,192,256]{3,2,1,0:T(8,128)(2,1)S(1)}, u32[]{:S(2)}, u32[]{:S(2)}) collective-permute-start(bf16[1,4,192,256]{3,2,1,0:T(8,128)(2,1)S(1)} %get-tuple-element.53), channel_id=1, source_target_pairs={{0,8},{8,16},{16,24},{24,0},{1,9},{9,17},{17,25},{25,1},{2,10},{10... | collective-permute-start | bytes 1179656 | tf_op jit(solution)/shard_map/ppermute | solution.py:28
  247.7 98.8 %collective-permute-start.7 = (bf16[1,4,192,256]{3,2,1,0:T(8,128)(2,1)S(1)}, bf16[1,4,192,256]{3,2,1,0:T(8,128)(2,1)S(1)}, u32[]{:S(2)}, u32[]{:S(2)}) collective-permute-start(bf16[1,4,192,256]{3,2,1,0:T(8,128)(2,1)S(1)} %get-tuple-element.52), channel_id=1, source_target_pairs={{0,16},{8,24},{16,0},{24,8},{1,17},{9,25},{17,1},{25,9},{2,18},{10... | collective-permute-start | bytes 1179656 | tf_op jit(solution)/shard_map/ppermute | solution.py:28
  314.1 32.4 %collective-permute-start.8 = (bf16[1,4,192,256]{3,2,1,0:T(8,128)(2,1)S(1)}, bf16[1,4,192,256]{3,2,1,0:T(8,128)(2,1)S(1)}, u32[]{:S(2)}, u32[]{:S(2)}) collective-permute-start(bf16[1,4,192,256]{3,2,1,0:T(8,128)(2,1)S(1)} %get-tuple-element.51), channel_id=1, source_target_pairs={{0,24},{8,0},{16,8},{24,16},{1,25},{9,1},{17,9},{25,17},{2,26},{10... | collective-permute-start | bytes 1179656 | tf_op jit(solution)/shard_map/ppermute | solution.py:28
  329.7 16.8 %copy-start.14 = (bf16[4,4,192,256]{3,2,1,0:T(8,128)(2,1)}, bf16[4,4,192,256]{3,2,1,0:T(8,128)(2,1)S(1)}, u32[]{:S(2)}) copy-start(bf16[4,4,192,256]{3,2,1,0:T(8,128)(2,1)S(1)} %constant_dynamic-update-slice_fusion.8) | copy-start | bytes 4718596
  409.5 8.4 %copy-start.9 = (bf16[1024,768]{1,0:T(8,128)(2,1)S(1)}, bf16[1024,768]{1,0:T(8,128)(2,1)}, u32[]{:S(2)}) copy-start(bf16[1024,768]{1,0:T(8,128)(2,1)} %copy-done.8) | copy-start | bytes 4718596
  409.5 92.5 %all-to-all-start.2 = ((bf16[1,4,1024,768]{3,1,0,2:T(4,128)(2,1)}), bf16[1,4,1024,768]{3,1,0,2:T(4,128)(2,1)}, u32[]{:S(2)}, u32[]{:S(2)}) async-start(bf16[1,4,1024,768]{3,1,0,2:T(4,128)(2,1)} %copy.104), calls=%async_computation.2 | async-start | bytes 12582912 | tf_op jit(solution)/shard_map/all_to_all | solution.py:324
  417.9 4.7 copy-start.21
  419.6 4.9 copy-start.11
  506.2 15.0 %copy-start.7 = (f32[4,4,64,768]{3,2,1,0:T(8,128)S(1)}, f32[4,4,64,768]{3,2,1,0:T(8,128)}, u32[]{:S(2)}) copy-start(f32[4,4,64,768]{3,2,1,0:T(8,128)} %copy.94) | copy-start | bytes 9437188
  (14 other events, 31.5 us)

commit v2 on v1

--- a/solution.py
+++ b/solution.py
@@ -281,6 +281,203 @@
     return (hidden.astype(jnp.float32) + ffn_out).astype(jnp.bfloat16)
 
 
+def moe_kernel(tp, ep, ff_tile, sent_ref, w_in_ref, w_out_ref, keys_ref, values_ref, back_ref, keys_out_ref, values_out_ref, turn_ref, relay_kv_ref, stage_ref, rows_ref, result_ref, relay_y_ref, relay_x_ref,
+               in_slots, out_slots, send_sem, recv_sem, weight_sem, local_sem):
+    me_tp, me_ep = lax.axis_index('tp'), lax.axis_index('ep')
+    right, left, across = lax.rem(me_tp + 1, tp), lax.rem(me_tp + tp - 1, tp), lax.rem(me_tp + 2, tp)
+
+    def partner_of(index):
+        return index + 1 - 2 * lax.rem(index, 2)
+
+    partner = partner_of(me_ep)
+    east, west, beyond = lax.rem(me_ep + 2, ep), lax.rem(me_ep + ep - 2, ep), lax.rem(me_ep + 4, ep)
+    east_other, west_other, beyond_other = partner_of(east), partner_of(west), partner_of(beyond)
+    peers = [{'tp': right}, {'tp': left}] + [{'ep': index} for index in (partner, east, east_other, west, west_other)]
+    to_right, to_left = peers[:2]
+
+    barrier = pltpu.get_barrier_semaphore()
+    for peer in peers:
+        pl.semaphore_signal(barrier, inc=1, device_id=peer, device_id_type=MESH)
+    pl.semaphore_wait(barrier, len(peers))
+
+    experts = w_in_ref.shape[0]
+    half_y, half_x = ep // 2, tp // 2
+    copies, local_copies = [], []
+
+    def send(source, target, peer):
+        index = len(copies)
+        copy = pltpu.make_async_remote_copy(src_ref=source, dst_ref=target, send_sem=send_sem.at[index], recv_sem=recv_sem.at[index],
+                                            device_id=peer, device_id_type=MESH)
+        copy.start()
+        copies.append(copy)
+        return copy
+
+    def keep(source, target):
+        copy = pltpu.make_async_copy(source, target, local_sem.at[len(local_copies)])
+        copy.start()
+        local_copies.append(copy)
+        return copy
+
+    def fetch(expert):
+        slot = expert % 2
+        pair = (pltpu.make_async_copy(w_in_ref.at[expert], in_slots.at[slot], weight_sem.at[slot, 0]),
+                pltpu.make_async_copy(w_out_ref.at[expert], out_slots.at[slot], weight_sem.at[slot, 1]))
+        for copy in pair:
+            copy.start()
+        return pair
+
+    class Exchange:
+        def __init__(self, way, expert, source, middle, target):
+            self.source, self.middle, self.target = source, middle, target
+            self.relay_y, self.relay_x = relay_y_ref.at[way, expert], relay_x_ref.at[way, expert]
+
+        def start_y(self):
+            self.hops = [send(self.source(across).at[0:half_y], self.relay_y.at[0], to_right),
+                         send(self.source(across).at[half_y:ep], self.relay_y.at[1], to_left)]
+            self.direct = [send(self.source(right), self.middle.at[me_tp], to_right), send(self.source(left), self.middle.at[me_tp], to_left)]
+            self.own = keep(self.source(me_tp), self.middle.at[me_tp])
+
+        def forward_y(self):
+            self.hops[0].wait_recv()
+            self.direct.append(send(self.relay_y.at[0], self.middle.at[left, 0:half_y], to_right))
+            self.hops[1].wait_recv()
+            self.direct.append(send(self.relay_y.at[1], self.middle.at[right, half_y:ep], to_left))
+
+        def finish_y(self):
+            for copy in self.direct:
+                copy.wait_recv()
+            self.own.wait()
+
+        def start_x(self):
+            self.hops, self.direct = [], []
+            for way, (near, low, high) in enumerate(((east, 0, half_x), (west, half_x, tp))):
+                for index, far in enumerate((beyond, beyond_other)):
+                    self.hops.append(send(self.middle.at[low:high, far], self.relay_x.at[way, index], {'ep': near}))
+            for near in (east, west, east_other, west_other, partner):
+                self.direct.append(send(self.middle.at[:, near], self.target(me_ep), {'ep': near}))
+
+        def forward_x(self):
+            for way, (origin, low, high, ends) in enumerate(((west, 0, half_x, (east, east_other)), (east, half_x, tp, (west, west_other)))):
+                for index, end in enumerate(ends):
+                    self.hops[2 * way + index].wait_recv()
+                    self.direct.append(send(self.relay_x.at[way, index], self.target(origin).at[low:high], {'ep': end}))
+
+        def finish_x(self):
+            for copy in self.direct:
+                copy.wait_recv()
+
+    def outward(expert):
+        return Exchange(0, expert, lambda index: sent_ref.at[index, :, expert], stage_ref.at[expert],
+                        lambda index: rows_ref.at[expert, :, index])
+
+    def inward(expert):
+        return Exchange(1, expert, lambda index: result_ref.at[expert, index], turn_ref.at[expert],
+                        lambda index: back_ref.at[:, index, expert])
+
+    def compute(expert, begin, end):
+        slot = expert % 2
+        if begin == 0:
+            for copy in weights[expert]:
+                copy.wait()
+            rows_ref[expert, :, me_ep] = stage_ref[expert, :, me_ep]
+        row_shape = rows_ref.shape[2:]
+        d_model, ff_dim = w_in_ref.shape[1:]
+
+        def one_tile(tile, carry):
+            rows = rows_ref[expert, tile].reshape(row_shape[0] * row_shape[1], row_shape[2])
+            total = None
+            for start in range(0, ff_dim, ff_tile):
+                pre = jnp.dot(rows, in_slots[slot, :, start:start + ff_tile], preferred_element_type=jnp.float32)
+                act = jax.nn.gelu(pre).astype(jnp.bfloat16)
+                part = jnp.dot(act, out_slots[slot, start:start + ff_tile], preferred_element_type=jnp.float32)
+                total = part if total is None else total + part
+            result_ref[expert, tile] = total.astype(jnp.bfloat16).reshape(row_shape)
+            return carry
+
+        lax.fori_loop(begin, end, one_tile, 0)
+
+    out = [outward(expert) for expert in range(experts)]
+    ret = [inward(expert) for expert in range(experts)]
+    chain = out + ret
+    weights = {}
+    last = len(chain) - 1
+    chain[0].start_y()
+    weights[0] = fetch(0)
+    weights[1] = fetch(1)
+    for step in range(last + 2):
+        expert = step - 2
+        if 0 <= expert < experts:
+            compute(expert, 0, 1)
+        if step <= last:
+            chain[step].forward_y()
+            if step < last:
+                chain[step + 1].start_y()
+        if step >= 1:
+            chain[step - 1].forward_x()
+        if 0 <= expert < experts:
+            compute(expert, 1, tp)
+            if expert + 2 < experts:
+                weights[expert + 2] = fetch(expert + 2)
+        if step <= last:
+            chain[step].finish_y()
+            chain[step].start_x()
+        if 1 <= step <= experts:
+            out[step - 1].finish_x()
+        if step == last - 1:
+            near_seqs = keys_ref.shape[1] // 2
+            spans = (slice(0, near_seqs), slice(near_seqs, 2 * near_seqs))
+            pairs = ((keys_ref, keys_out_ref), (values_ref, values_out_ref))
+            cache_own = [keep(source.at[me_tp], target.at[me_tp]) for source, target in pairs]
+        if step == last:
+            cache_hops = [send(source.at[across, spans[way]], relay_kv_ref.at[index, way], peer)
+                          for index, (source, _) in enumerate(pairs) for way, peer in enumerate((to_right, to_left))]
+            cache_moves = [send(source.at[goal], target.at[me_tp], peer)
+                           for source, target in pairs for goal, peer in ((right, to_right), (left, to_left))]
+    own = [keep(turn_ref.at[expert, :, me_ep], back_ref.at[:, me_ep, expert]) for expert in range(experts)]
+    for index, (_, target) in enumerate(pairs):
+        for way, (origin, peer) in enumerate(((left, to_right), (right, to_left))):
+            cache_hops[2 * index + way].wait_recv()
+            cache_moves.append(send(relay_kv_ref.at[index, way], target.at[origin, spans[way]], peer))
+    for exchange in ret:
+        exchange.finish_x()
+    for copy in cache_moves:
+        copy.wait_recv()
+    for copy in cache_own:
+        copy.wait()
+    for copy in own:
+        copy.wait()
+    for copy in copies:
+        copy.wait_send()
+
+
+def moe_exchange(dispatched, expert_in, expert_out, keys, values, tp, ep):
+    experts, d_model, ff_dim = expert_in.shape
+    slots = dispatched.shape[0] // (tp * ep * experts)
+    view = dispatched.reshape(tp, ep, experts, slots, d_model)
+    any_spec = pl.BlockSpec(memory_space=pl.ANY)
+    rows = (experts, tp, ep, slots, d_model)
+    count = experts * 2 * (6 + 13) + 12
+    cache = jax.ShapeDtypeStruct(keys.shape, keys.dtype)
+    relay = jax.ShapeDtypeStruct((2, 2, keys.shape[1] // 2) + keys.shape[2:], keys.dtype)
+    dtype = dispatched.dtype
+    total_rows = dispatched.shape[0]
+    back, keys, values, _, _ = pl.pallas_call(
+        functools.partial(moe_kernel, tp, ep, ff_dim // 4),
+        in_specs=[any_spec] * 5,
+        out_specs=[any_spec] * 5,
+        out_shape=[jax.ShapeDtypeStruct(view.shape, dtype), cache, cache, jax.ShapeDtypeStruct(rows, dtype), relay],
+        scratch_shapes=[pltpu.VMEM(rows, dtype), pltpu.VMEM(rows, dtype), pltpu.VMEM(rows, dtype),
+                        pltpu.VMEM((2, experts, 2, ep // 2, slots, d_model), dtype), pltpu.VMEM((2, experts, 2, 2, tp // 2, slots, d_model), dtype),
+                        pltpu.VMEM((2, d_model, ff_dim), dtype), pltpu.VMEM((2, ff_dim, d_model), dtype),
+                        pltpu.SemaphoreType.DMA((count,)), pltpu.SemaphoreType.DMA((count,)), pltpu.SemaphoreType.DMA((2, 2)),
+                        pltpu.SemaphoreType.DMA((3 * experts + 2,))],
+        compiler_params=pltpu.CompilerParams(collective_id=1, has_side_effects=True, vmem_limit_bytes=62 * 1024 * 1024),
+        cost_estimate=pl.CostEstimate(flops=4 * total_rows * d_model * ff_dim, bytes_accessed=4 * expert_in.size, transcendentals=0),
+        name='moe_exchange',
+    )(view, expert_in, expert_out, keys, values)
+    return back.reshape(dispatched.shape), keys, values
+
+
 def slot_table(choices, num_experts):
     experts = jnp.arange(num_experts, dtype=jnp.int32)
     first_hot = (choices[..., 0:1] == experts).astype(jnp.int32)
@@ -291,12 +488,10 @@
     return jnp.stack([first_pos, second_pos], axis=-1)
 
 
-def moe_block(hidden, ln_scale, w_router, expert_in, expert_out, expert_ids, caches):
+def moe_block(hidden, ln_scale, w_router, expert_in, expert_out, expert_ids, caches, tp, ep):
     local_batch, local_seq, d_model = hidden.shape
     tokens = local_batch * local_seq
     num_experts = w_router.shape[1]
-    local_experts = expert_in.shape[0]
-    groups = num_experts // local_experts
     capacity = 4 * tokens // num_experts
     choices = expert_ids.reshape(tokens, 2)
     position = slot_table(choices, num_experts)
@@ -306,9 +501,7 @@
 
     normed = rms_norm(hidden, ln_scale).reshape(tokens, d_model)
     dispatched = jnp.einsum('ncs,nd->sd', select, normed, preferred_element_type=jnp.float32).astype(jnp.bfloat16)
-    dispatched = dispatched.reshape(groups, local_experts, capacity, d_model)
-    received = lax.all_to_all(dispatched, GROUP, 0, 2, tiled=True)
-    expert_rows = received.reshape(local_experts, groups * capacity, d_model)
+    returned, *caches = moe_exchange(dispatched, expert_in, expert_out, *caches, tp, ep)
 
     logits = jnp.dot(normed.astype(jnp.float32), w_router, precision=lax.Precision.HIGHEST)
     router_probs = jax.nn.softmax(logits, axis=-1)
@@ -316,13 +509,6 @@
     picked = jnp.sum(jnp.where(choices[:, :, None] == experts, router_probs[:, None, :], 0.0), axis=-1)
     gate_weights = picked / jnp.sum(picked, axis=-1, keepdims=True)
 
-    expert_hidden = jnp.einsum('erd,edf->erf', expert_rows, expert_in, preferred_element_type=jnp.float32)
-    expert_hidden = jax.nn.gelu(expert_hidden).astype(jnp.bfloat16)
-    expert_result = jnp.einsum('erf,efd->erd', expert_hidden, expert_out, preferred_element_type=jnp.float32).astype(jnp.bfloat16)
-    expert_result, *caches = lax.optimization_barrier((expert_result, *caches))
-    expert_result = expert_result.reshape(1, local_experts, groups * capacity, d_model)
-    returned = lax.all_to_all(expert_result, GROUP, 2, 0, tiled=True)
-    returned = returned.reshape(num_experts * capacity, d_model)
     gathered_out = jnp.einsum('ncs,sd->ncd', select, returned, preferred_element_type=jnp.float32)
     moe_sum = jnp.sum(gate_weights[:, :, None] * gathered_out, axis=1).reshape(local_batch, local_seq, d_model)
     return (hidden.astype(jnp.float32) + moe_sum).astype(jnp.bfloat16), *caches
@@ -338,8 +524,7 @@
     in_specs = (act_spec, P(), P(), col_spec, col_spec, col_spec, row_spec, row_spec,
                 P(None, 'tp'), P(None, 'tp'), P('tp', None), P(), expert_spec, expert_spec, act_spec)
 
-    def to_owner(blocks, local_heads):
-        got = tp_exchange_permutes(blocks, tp)
+    def as_cache(got, local_heads):
         return jnp.swapaxes(got.reshape(got.shape[0] * got.shape[1], local_heads, -1, got.shape[3]), 2, 3)
 
     def device_fn(hidden_in, ln_attn, ln_ffn, w_query, w_key, w_value, w_out, bias_table, w_gate, w_up, w_down, w_router, expert_in, expert_out, expert_ids):
@@ -351,14 +536,14 @@
         blocks = [packed(0), w_up, w_down, packed(1), w_gate]
         hidden, tables, (attn_zero, up, down, attn_one, gate) = gather_all(hidden_in, bias_table, blocks, len(blocks) - 1, tp, ep)
         hidden, keys_zero, values_zero = attention(hidden, ln_attn[0], attn_zero, tables[0], tp)
-        keys_zero, values_zero = to_owner(keys_zero, local_heads), to_owner(values_zero, local_heads)
+        keys_zero, values_zero = tp_exchange_permutes(keys_zero, tp), tp_exchange_permutes(values_zero, tp)
         hidden = dense_ffn(hidden, ln_ffn[0], gate, up, down)
         hidden, keys_one, values_one = attention(hidden, ln_attn[1], attn_one, tables[1], tp)
         hidden, keys_zero, values_zero = lax.optimization_barrier((hidden, keys_zero, values_zero))
-        keys_one, values_one = to_owner(keys_one, local_heads), to_owner(values_one, local_heads)
         hidden = lax.all_to_all(hidden, 'tp', 1, 0, tiled=True)
-        hidden, keys_one, values_one = moe_block(hidden, ln_ffn[1], w_router, expert_in, expert_out, expert_ids, (keys_one, values_one))
-        keys, values = jnp.stack([keys_zero, keys_one]), jnp.stack([values_zero, values_one])
+        hidden, keys_one, values_one = moe_block(hidden, ln_ffn[1], w_router, expert_in, expert_out, expert_ids, (keys_one, values_one), tp, ep)
+        keys = jnp.stack([as_cache(keys_zero, local_heads), as_cache(keys_one, local_heads)])
+        values = jnp.stack([as_cache(values_zero, local_heads), as_cache(values_one, local_heads)])
         return hidden, keys, values
 
     return jax.shard_map(device_fn, mesh=mesh, in_specs=in_specs, out_specs=(act_spec, cache_spec, cache_spec), check_vma=False)

time: 530 us -> 467 us (0.88)
  the two profiles are of different devices: /device:TPU:103 before, /device:TPU:97 now
where the time goes in v2:
time: 467 us; the launch traced here: 460 us
  Pallas kernels  304 us (65%)
  matrix products  60.9 us (13%)
  local copies, waits for them, and re-layouts  47.7 us (10%)
  other arithmetic  32.9 us (7%)
  starting transfers between devices  11.4 us (2%)
    pallas_call x1, Pallas kernels, moe_exchange(): pl.pallas_call(functools.partial(moe_kernel, tp, ep, ff_dim // 4), in_spe...  181 us
    pallas_call x1, Pallas kernels, gather_all(): pl.pallas_call(functools.partial(gather_kernel, tp, ep, num_blocks, direc...  76.4 us
    pallas_call x2, Pallas kernels, attention(): pl.pallas_call(functools.partial(attention_kernel, tp), grid=(seqs,), in_...  46.3 us
    dot_general x1, matrix products, dense_ffn(): jnp.einsum('stgf,gfd->std', ffn_hidden, down, preferred_element_type=jnp....  18.7 us
    dot_general x1, matrix products, moe_block(): jnp.einsum('ncs,sd->ncd', select, returned, preferred_element_type=jnp.fl...  17.8 us
    unnamed x58, local copies, waits for them, and re-layouts  17.2 us
    reduce_sum x1, other arithmetic, moe_block(): jnp.einsum('ncs,nd->sd', select, normed, preferred_element_type=jnp.float32)  13.8 us
    dot_general x1, matrix products, moe_block(): jnp.einsum('ncs,nd->sd', select, normed, preferred_element_type=jnp.float32)  12.3 us
  transfers between devices with their start and end apart: 7, of which 2 were waited for; matrix products, arithmetic and copies ran while one was open for 15% of the time, Pallas kernels for 5%

profile of v2, /device:TPU:97, one launch (start us, length us, event | category | flops | bytes accessed | tf_op | source)
XLA Modules:
  0.0 460.0 jit_solution(8945992721291197952)
XLA Ops:
  4.7 1.6 pad_maximum_fusion.2
  6.3 76.4 %gather_all.1 = (bf16[4,4,64,768]{3,2,1,0:T(8,128)(2,1)}, bf16[2,2,64,768]{3,2,1,0:T(8,128)(2,1)}, f32[4,2,3,32]{3,2,1,0:T(4,128)}, bf16[4,8,96,768]{3,2,1,0:T(8...) custom-call(bf16[4,4,64,768]{3,2,1,0:T(8,128)(2,1)} %bitcast.141, ...), custom_call_target="tpu_custom_call" | custom-call | tf_op jit(solution)/shard_map/gather_all/pallas_call | solution.py:168
  84.1 2.3 copy-done.3
  86.4 1.4 copy-done.4
  87.8 22.9 %attention.2 = (bf16[4,256,768]{2,1,0:T(8,128)(2,1)S(1)}, bf16[4,4,192,256]{3,2,1,0:T(8,128)(2,1)S(1)}, bf16[4,4,192,256]{3,2,1,0:T(8,128)(2,1)S(1)}) custom-call(bf16[4,256,768]{2,1,0:T(8,128)(2,1)S(1)} %bitcast.133, f32[1,768]{1,0:T(1,128)S(1)} %get-tuple-element.68.ln_ref, bf16[4,768,768]{2,1,0:T(8,128)(2,1)S(1)} %bitcast.132, f32[12,32]{1,0:T(8,128)S(1)} %squeeze.38.table_ref), custom_call_target="tpu_custom_call" | custom-call | flops 7247757312 | bytes 11010048 | tf_op jit(solution)/shard_map/attention/pallas_call | solution.py:259
  113.8 1.8 collective-permute-start.5
  117.0 1.5 collective-permute-start.1
  122.2 1.4 eq.91
  123.6 1.4 fusion.51
  124.9 1.4 copy.84
  130.7 1.9 add_add_fusion.1
  133.3 10.5 %fusion.28 = f32[4,256,4,768]{3,1,2,0:T(8,128)} fusion(bf16[4,768,768,1]{2,1,0,3:T(8,128)(2,1)} %bitcast.157, bf16[4,256,768]{2,1,0:T(8,128)(2,1)S(1)} %get-tuple-element.25, f32[768]{0:T(1024)} %get-tuple-element.44, f32[4,256]{1,0:T(4,128)} %add_rsqrt_fusion.1), kind=kOutput, calls=%fused_computation.35 | convolution fusion | flops 4834983936 | bytes 18881536 | tf_op jit(solution)/shard_map/std,gdf->stgf/dot_general | solution.py:277
  143.8 18.7 %fusion.17.hidden_ref = bf16[4,256,768]{2,1,0:T(8,128)(2,1)} fusion(bf16[4,256,768]{2,1,0:T(8,128)(2,1)S(1)} %get-tuple-element.25, bf16[4,768,768,1]{2,1,0,3:T(8,128)(2,1)} %bitcast.156, f32[4,256,4,768]{3,1,2,0:T(8,128)} %fusion.28, bf16[4,768,768,1]{2,1,0,3:T(8,128)(2,1)} %bitcast.155, f32[768]{0:T(1024)} %get-tuple-element.44, f32[4,256]{1,0:T(4,128)} %add_rsqrt_fusion.1), kind=kOutput, calls=%fused_computation.24 | convolution fusion | flops 9700638720 | bytes 25172992 | tf_op jit(solution)/shard_map/stgf,gfd->std/dot_general | solution.py:280
  162.5 2.3 copy-done.2
  164.8 1.4 copy-done.7
  166.2 23.4 %attention.3 = (bf16[4,256,768]{2,1,0:T(8,128)(2,1)S(1)}, bf16[4,4,192,256]{3,2,1,0:T(8,128)(2,1)S(1)}, bf16[4,4,192,256]{3,2,1,0:T(8,128)(2,1)S(1)}) custom-call(bf16[4,256,768]{2,1,0:T(8,128)(2,1)S(1)} %copy-done.7, f32[1,768]{1,0:T(1,128)S(1)} %get-tuple-element.67.ln_ref, bf16[4,768,768]{2,1,0:T(8,128)(2,1)S(1)} %bitcast.131, f32[12,32]{1,0:T(8,128)S(1)} %squeeze.39.table_ref), custom_call_target="tpu_custom_call" | custom-call | flops 7247757312 | bytes 11010048 | tf_op jit(solution)/shard_map/attention/pallas_call | solution.py:259
  194.4 1.9 collective-permute-start.2
  196.4 1.8 constant_dynamic-update-slice_fusion.2
  198.1 1.8 constant_dynamic-update-slice_fusion.1
  199.9 1.8 constant_dynamic-update-slice_fusion
  204.3 2.4 copy.77
  206.6 4.1 all-to-all-start
  211.9 1.4 fusion.36
  213.7 13.8 %convert_reduce_fusion = bf16[1024,4096]{1,0:T(8,128)(2,1)} fusion(s32[1024,2]{0,1:T(2,128)S(1)} %compare_select_fusion), kind=kLoop, calls=%fused_computation | loop fusion | flops 29360128 | bytes 8396800 | tf_op jit(solution)/shard_map/ncs,nd->sd/reduce_sum | solution.py:503
  235.2 1.4 rsqrt.21
  237.6 12.3 %fusion.54 = bf16[4096,768]{1,0:T(8,128)(2,1)} fusion(bf16[1024,4096]{1,0:T(8,128)(2,1)} %convert_reduce_fusion, bf16[1024,768]{1,0:T(8,128)(2,1)S(1)} %fusion.19), kind=kOutput, calls=%fused_computation.105 | convolution fusion | flops 6442450944 | bytes 16252928 | tf_op jit(solution)/shard_map/ncs,nd->sd/dot_general | solution.py:503
  249.9 1.7 fusion.53
  253.1 181.2 %moe_exchange.1 = (bf16[4,8,4,32,768]{4,3,2,1,0:T(8,128)(2,1)}, bf16[4,4,192,256]{3,2,1,0:T(8,128)(2,1)}, bf16[4,4,192,256]{3,2,1,0:T(8,128)(2,1)}, bf16[4,4,8,3...) custom-call(bf16[4,8,4,32,768]{4,3,2,1,0:T(8,128)(2,1)} %bitcast.158, bf16[4,768,3072]{2,1,0:T(8,128)(2,1)} %w_in_ref.1, ...), custom_call_target="tpu_custom_call" | custom-call | flops 38654705664 | bytes 37748736 | tf_op jit(solution)/shard_map/moe_exchange/pallas_call | solution.py:464
  434.3 17.8 %multiply_reduce_fusion = f32[1024,768]{1,0:T(8,128)S(1)} fusion(f32[1024,2]{0,1:T(2,128)S(1)} %broadcast_divide_fusion, bf16[4096,768,1]{1,0,2:T(8,128)(2,1)} %bitcast.159, s32[1024,2]{0,1:T(2,128)S(1)} %compare_select_fusion), kind=kOutput, calls=%fused_computation.16 | convolution fusion | flops 12895649792 | bytes 9453568 | tf_op jit(solution)/shard_map/ncs,sd->ncd/dot_general | solution.py:512
  452.1 1.6 fusion.20
  454.6 1.9 pad_maximum_fusion.1
  457.6 1.9 pad_maximum_fusion
  (108 shorter events, 39.5 us)
Async XLA Ops:
  0.6 249.3 %copy-start = (f32[768,128]{1,0:T(8,128)S(1)}, f32[768,128]{1,0:T(8,128)}, u32[]{:S(2)}) copy-start(f32[768,128]{1,0:T(8,128)} %param.26) | copy-start | bytes 1179652
  0.6 3.4 copy-start.21
  0.7 3.5 copy-start.27
  6.3 77.7 %copy-start.26 = (f32[2,768]{1,0:T(2,128)S(1)}, f32[2,768]{1,0:T(2,128)}, u32[]{:S(2)}) copy-start(f32[2,768]{1,0:T(2,128)} %param.16) | copy-start | bytes 18436
  84.1 2.3 copy-start.3
  86.4 1.4 copy-start.4
  112.0 7.0 %copy-start.14 = (bf16[4,4,192,256]{3,2,1,0:T(8,128)(2,1)}, bf16[4,4,192,256]{3,2,1,0:T(8,128)(2,1)S(1)}, u32[]{:S(2)}) copy-start(bf16[4,4,192,256]{3,2,1,0:T(8,128)(2,1)S(1)} %get-tuple-element.50) | copy-start | bytes 4718596
  112.0 82.5 %collective-permute-start.3 = (bf16[1,4,192,256]{3,2,1,0:T(8,128)(2,1)}, bf16[1,4,192,256]{3,2,1,0:T(8,128)(2,1)}, u32[]{:S(2)}, u32[]{:S(2)}) collective-permute-start(bf16[1,4,192,256]{3,2,1,0:T(8,128)(2,1)} %get-tuple-element.49), channel_id=1, source_target_pairs={{0,8},{8,16},{16,24},{24,0},{1,9},{9,17},{17,25},{25,1},{2,10},{10... | collective-permute-start | bytes 1179656 | tf_op jit(solution)/shard_map/ppermute | solution.py:28
  112.6 85.5 %collective-permute-start.4 = (bf16[1,4,192,256]{3,2,1,0:T(8,128)(2,1)}, bf16[1,4,192,256]{3,2,1,0:T(8,128)(2,1)}, u32[]{:S(2)}, u32[]{:S(2)}) collective-permute-start(bf16[1,4,192,256]{3,2,1,0:T(8,128)(2,1)} %get-tuple-element.48), channel_id=1, source_target_pairs={{0,16},{8,24},{16,0},{24,8},{1,17},{9,25},{17,1},{25,9},{2,18},{10... | collective-permute-start | bytes 1179656 | tf_op jit(solution)/shard_map/ppermute | solution.py:28
  113.8 86.1 %collective-permute-start.5 = (bf16[1,4,192,256]{3,2,1,0:T(8,128)(2,1)}, bf16[1,4,192,256]{3,2,1,0:T(8,128)(2,1)}, u32[]{:S(2)}, u32[]{:S(2)}) collective-permute-start(bf16[1,4,192,256]{3,2,1,0:T(8,128)(2,1)} %get-tuple-element.47), channel_id=1, source_target_pairs={{0,24},{8,0},{16,8},{24,16},{1,25},{9,1},{17,9},{25,17},{2,26},{10... | collective-permute-start | bytes 1179656 | tf_op jit(solution)/shard_map/ppermute | solution.py:28
  115.6 4.0 copy-start.25
  116.8 84.9 %collective-permute-start = (bf16[1,4,192,256]{3,2,1,0:T(8,128)(2,1)}, bf16[1,4,192,256]{3,2,1,0:T(8,128)(2,1)}, u32[]{:S(2)}, u32[]{:S(2)}) collective-permute-start(bf16[1,4,192,256]{3,2,1,0:T(8,128)(2,1)} %get-tuple-element.53), channel_id=1, source_target_pairs={{0,8},{8,16},{16,24},{24,0},{1,9},{9,17},{17,25},{25,1},{2,10},{10... | collective-permute-start | bytes 1179656 | tf_op jit(solution)/shard_map/ppermute | solution.py:28
  117.0 85.7 %collective-permute-start.1 = (bf16[1,4,192,256]{3,2,1,0:T(8,128)(2,1)}, bf16[1,4,192,256]{3,2,1,0:T(8,128)(2,1)}, u32[]{:S(2)}, u32[]{:S(2)}) collective-permute-start(bf16[1,4,192,256]{3,2,1,0:T(8,128)(2,1)} %get-tuple-element.52), channel_id=1, source_target_pairs={{0,16},{8,24},{16,0},{24,8},{1,17},{9,25},{17,1},{25,9},{2,18},{10... | collective-permute-start | bytes 1179656 | tf_op jit(solution)/shard_map/ppermute | solution.py:28
  162.5 2.3 copy-start.2
  164.8 1.4 copy-start.7
  166.2 25.7 %copy-start.22 = (s32[8,128]{0,1:T(8,128)S(1)}, s32[8,128]{0,1:T(8,128)}, u32[]{:S(2)}) copy-start(s32[8,128]{0,1:T(8,128)} %copy.86) | copy-start | bytes 12292
  166.2 26.7 %copy-start.18 = (s32[128,8,128]{0,1,2:T(8,128)S(1)}, s32[128,8,128]{0,1,2:T(8,128)}, u32[]{:S(2)}) copy-start(s32[128,8,128]{0,1,2:T(8,128)} %add_add_fusion.1) | copy-start | bytes 1572868
  189.6 1.1 copy-start.5
  190.7 1.2 copy-start.6
  194.4 9.8 %collective-permute-start.2 = (bf16[1,4,192,256]{3,2,1,0:T(8,128)(2,1)}, bf16[1,4,192,256]{3,2,1,0:T(8,128)(2,1)S(1)}, u32[]{:S(2)}, u32[]{:S(2)}) collective-permute-start(bf16[1,4,192,256]{3,2,1,0:T(8,128)(2,1)} %get-tuple-element.51), channel_id=1, source_target_pairs={{0,24},{8,0},{16,8},{24,16},{1,25},{9,1},{17,9},{25,17},{2,26},{10... | collective-permute-start | bytes 1179656 | tf_op jit(solution)/shard_map/ppermute | solution.py:28
  204.3 2.4 copy-start.12
  206.6 5.3 %copy-start.24 = (s32[1024,1]{0,1:T(1,128)S(1)}, s32[1024,1]{0,1:T(1,128)}, u32[]{:S(2)}) copy-start(s32[1024,1]{0,1:T(1,128)} %get-tuple-element.65) | copy-start | bytes 12292
  206.6 7.1 %copy-start.23 = (s32[1024,2]{0,1:T(2,128)S(1)}, s32[1024,2]{0,1:T(2,128)}, u32[]{:S(2)}) copy-start(s32[1024,2]{0,1:T(2,128)} %eq.91) | copy-start | bytes 24580
  206.6 22.2 %all-to-all-start = ((bf16[4,256,768]{2,0,1:T(4,128)(2,1)}), bf16[4,256,768]{2,0,1:T(4,128)(2,1)S(1)}, u32[]{:S(2)}, u32[]{:S(2)}) async-start(bf16[4,256,768]{2,0,1:T(4,128)(2,1)} %copy.77), calls=%async_computation | async-start | bytes 3145728 | tf_op jit(solution)/shard_map/all_to_all | solution.py:543
  229.9 1.4 copy-start.11
  231.3 6.3 %copy-start.8 = (f32[4,4,64,768]{3,2,1,0:T(8,128)}, f32[4,4,64,768]{3,2,1,0:T(8,128)S(1)}, u32[]{:S(2)}) copy-start(f32[4,4,64,768]{3,2,1,0:T(8,128)S(1)} %copy.79) | copy-start | bytes 9437188
  434.3 17.8 %copy-start.9 = (f32[4,4,64,768]{3,2,1,0:T(8,128)S(1)}, f32[4,4,64,768]{3,2,1,0:T(8,128)}, u32[]{:S(2)}) copy-start(f32[4,4,64,768]{3,2,1,0:T(8,128)} %copy-done.8) | copy-start | bytes 9437188
  452.1 1.7 copy-start.15
  452.1 2.4 copy-start.20
  454.6 1.9 copy-start.13
  454.6 3.0 copy-start.19
  456.5 3.0 copy-start.1
  (3 other events, 2.7 us)

commit v3 on v2

--- a/solution.py
+++ b/solution.py
@@ -18,16 +18,6 @@
     wide_rows = rows_in.astype(jnp.float32)
     inv_rms = lax.rsqrt(jnp.mean(wide_rows * wide_rows, axis=-1, keepdims=True) + EPSILON)
     return (wide_rows * inv_rms * ln_scale).astype(jnp.bfloat16)
-
-
-def tp_exchange_permutes(blocks, tp):
-    me = lax.axis_index('tp')
-    out = lax.dynamic_update_index_in_dim(jnp.zeros_like(blocks), lax.dynamic_index_in_dim(blocks, me, 0), me, 0)
-    for step in range(1, tp):
-        block = lax.dynamic_index_in_dim(blocks, (me + step) % tp, 0)
-        got = lax.ppermute(block, 'tp', [(i, (i + step) % tp) for i in range(tp)])
-        out = lax.dynamic_update_index_in_dim(out, got, (me + tp - step) % tp, 0)
-    return out
 
 
 def gather_kernel(tp, ep, num_blocks, direct, hidden_ref, table_ref, *refs):
@@ -184,13 +174,54 @@
     return hidden, tables, [block.reshape(tp, -1, d_model) for block in results[3:]]
 
 
-def attention_kernel(tp, hidden_ref, ln_ref, w_ref, table_ref, out_ref, keys_ref, values_ref, bias_ref, q_ref, kt_ref, ctx_ref, w_out_ref):
+def attention_kernel(tp, moving, hidden_ref, ln_ref, w_ref, table_ref, *refs):
+    if moving:
+        old_keys_ref, old_values_ref, out_ref, keys_ref, values_ref, new_keys_ref, new_values_ref = refs[:7]
+        relay_ref, send_sem, recv_sem, local_sem = refs[12:]
+        bias_ref, q_ref, kt_ref, ctx_ref, w_out_ref = refs[7:12]
+    else:
+        out_ref, keys_ref, values_ref, bias_ref, q_ref, kt_ref, ctx_ref, w_out_ref = refs
     seq_len, d_model = hidden_ref.shape[1], hidden_ref.shape[2]
     num_heads = table_ref.shape[0]
     head_dim = d_model // num_heads
     half = seq_len // 2
     width = d_model // tp
     starts = tuple(range(EXACT_BUCKETS + 1)) + THRESHOLDS
+
+    if moving:
+        me_tp = lax.axis_index('tp')
+        right, left, across = lax.rem(me_tp + 1, tp), lax.rem(me_tp + tp - 1, tp), lax.rem(me_tp + 2, tp)
+        pairs = ((old_keys_ref, new_keys_ref), (old_values_ref, new_values_ref))
+        half_seqs = old_keys_ref.shape[1] // 2
+        spans = (slice(0, half_seqs), slice(half_seqs, 2 * half_seqs))
+
+        def remote(index, source, target, to):
+            return pltpu.make_async_remote_copy(src_ref=source, dst_ref=target, send_sem=send_sem.at[index], recv_sem=recv_sem.at[index],
+                                                device_id={'tp': to}, device_id_type=MESH)
+
+        hops, directs, forwards, owns = [], [], [], []
+        for index, (source, target) in enumerate(pairs):
+            for way, (goal, origin) in enumerate(((right, left), (left, right))):
+                number = 2 * index + way
+                hops.append(remote(number, source.at[across, spans[way]], relay_ref.at[index, way], goal))
+                directs.append(remote(4 + number, source.at[goal], target.at[me_tp], goal))
+                forwards.append(remote(8 + number, relay_ref.at[index, way], target.at[origin, spans[way]], goal))
+            owns.append(pltpu.make_async_copy(source.at[me_tp], target.at[me_tp], local_sem.at[index]))
+
+        @pl.when(pl.program_id(0) == 0)
+        def _():
+            barrier = pltpu.get_barrier_semaphore()
+            for goal in (right, left):
+                pl.semaphore_signal(barrier, inc=1, device_id={'tp': goal}, device_id_type=MESH)
+            pl.semaphore_wait(barrier, 2)
+            for copy in hops + directs + owns:
+                copy.start()
+
+        @pl.when(pl.program_id(0) == 2)
+        def _():
+            for hop, forward in zip(hops, forwards):
+                hop.wait_recv()
+                forward.start()
 
     @pl.when(pl.program_id(0) == 0)
     def _():
@@ -247,8 +278,18 @@
     attn_out = jnp.dot(ctx_ref[...].T, w_out_ref[...], preferred_element_type=jnp.float32)
     out_ref[0] = (rows + attn_out).astype(jnp.bfloat16)
 
-
-def attention(hidden, ln_scale, packed, table, tp):
+    if moving:
+        @pl.when(pl.program_id(0) == pl.num_programs(0) - 1)
+        def _():
+            for copy in directs + forwards:
+                copy.wait_recv()
+            for copy in hops + directs + forwards:
+                copy.wait_send()
+            for copy in owns:
+                copy.wait()
+
+
+def attention(hidden, ln_scale, packed, table, tp, old=()):
     seqs, seq_len, d_model = hidden.shape
     num_heads = table.shape[0]
     width = d_model // tp
@@ -256,20 +297,27 @@
     cache_block = pl.BlockSpec((tp, 1, width, seq_len), lambda s: (0, s, 0, 0))
     cache = jax.ShapeDtypeStruct((tp, seqs, width, seq_len), jnp.bfloat16)
     flops = 2 * seqs * seq_len * d_model * (5 * d_model + 3 * seq_len)
+    any_spec = pl.BlockSpec(memory_space=pl.ANY)
+    scratch = [pltpu.VMEM((num_heads, seq_len // 2, seq_len), jnp.float32), pltpu.VMEM((d_model, seq_len), jnp.bfloat16),
+               pltpu.VMEM((d_model, seq_len), jnp.bfloat16), pltpu.VMEM((d_model, seq_len), jnp.bfloat16),
+               pltpu.VMEM((d_model, d_model), jnp.bfloat16)]
+    options = {}
+    if old:
+        scratch += [pltpu.VMEM((2, 2, seqs // 2) + cache.shape[2:], jnp.bfloat16), pltpu.SemaphoreType.DMA((12,)),
+                    pltpu.SemaphoreType.DMA((12,)), pltpu.SemaphoreType.DMA((2,))]
+        options = dict(collective_id=2, has_side_effects=True)
     return pl.pallas_call(
-        functools.partial(attention_kernel, tp),
+        functools.partial(attention_kernel, tp, bool(old)),
         grid=(seqs,),
         in_specs=[seq_block, pl.BlockSpec((1, d_model), lambda s: (0, 0)), pl.BlockSpec((tp, d_model, d_model), lambda s: (0, 0, 0)),
-                  pl.BlockSpec(memory_space=pltpu.SMEM)],
-        out_specs=[seq_block, cache_block, cache_block],
-        out_shape=[jax.ShapeDtypeStruct(hidden.shape, hidden.dtype), cache, cache],
-        scratch_shapes=[pltpu.VMEM((num_heads, seq_len // 2, seq_len), jnp.float32), pltpu.VMEM((d_model, seq_len), jnp.bfloat16),
-                        pltpu.VMEM((d_model, seq_len), jnp.bfloat16), pltpu.VMEM((d_model, seq_len), jnp.bfloat16),
-                        pltpu.VMEM((d_model, d_model), jnp.bfloat16)],
-        compiler_params=pltpu.CompilerParams(dimension_semantics=('arbitrary',), vmem_limit_bytes=40 * 1024 * 1024),
+                  pl.BlockSpec(memory_space=pltpu.SMEM)] + [any_spec] * len(old),
+        out_specs=[seq_block, cache_block, cache_block] + [any_spec] * len(old),
+        out_shape=[jax.ShapeDtypeStruct(hidden.shape, hidden.dtype), cache, cache] + [cache] * len(old),
+        scratch_shapes=scratch,
+        compiler_params=pltpu.CompilerParams(dimension_semantics=('arbitrary',), vmem_limit_bytes=40 * 1024 * 1024, **options),
         cost_estimate=pl.CostEstimate(flops=flops, bytes_accessed=2 * (hidden.size * 4 + packed.size), transcendentals=0),
-        name='attention',
-    )(hidden, ln_scale[None], packed, table)
+        name='attention_moving' if old else 'attention',
+    )(hidden, ln_scale[None], packed, table, *old)
 
 
 def dense_ffn(hidden, ln_scale, gate, up, down):
@@ -478,6 +526,36 @@
     return back.reshape(dispatched.shape), keys, values
 
 
+def dispatch_kernel(hidden_ref, ln_ref, ids_ref, out_ref, normed_ref):
+    @pl.when(pl.program_id(0) == 0)
+    def _():
+        rows = hidden_ref[...].astype(jnp.float32)
+        inv_rms = lax.rsqrt(jnp.mean(rows * rows, axis=-1, keepdims=True) + EPSILON)
+        normed_ref[...] = (rows * inv_rms * ln_ref[...]).astype(jnp.bfloat16)
+
+    slots = lax.broadcasted_iota(jnp.int32, (out_ref.shape[0], hidden_ref.shape[0]), 0) + pl.program_id(0) * out_ref.shape[0]
+    hit = (ids_ref[0:1] == slots) | (ids_ref[1:2] == slots)
+    select = jnp.where(hit, 1.0, 0.0).astype(jnp.bfloat16)
+    out_ref[...] = jnp.dot(select, normed_ref[...], preferred_element_type=jnp.float32).astype(jnp.bfloat16)
+
+
+def dispatch(rows, ln_scale, slot_ids, num_slots):
+    tokens, d_model = rows.shape
+    block = num_slots // 8
+    return pl.pallas_call(
+        dispatch_kernel,
+        grid=(num_slots // block,),
+        in_specs=[pl.BlockSpec((tokens, d_model), lambda s: (0, 0)), pl.BlockSpec((1, d_model), lambda s: (0, 0)),
+                  pl.BlockSpec((2, tokens), lambda s: (0, 0))],
+        out_specs=pl.BlockSpec((block, d_model), lambda s: (s, 0)),
+        out_shape=jax.ShapeDtypeStruct((num_slots, d_model), jnp.bfloat16),
+        scratch_shapes=[pltpu.VMEM((tokens, d_model), jnp.bfloat16)],
+        compiler_params=pltpu.CompilerParams(dimension_semantics=('arbitrary',), vmem_limit_bytes=32 * 1024 * 1024),
+        cost_estimate=pl.CostEstimate(flops=2 * tokens * num_slots * d_model, bytes_accessed=2 * num_slots * d_model, transcendentals=0),
+        name='dispatch',
+    )(rows, ln_scale[None], jnp.swapaxes(slot_ids, 0, 1))
+
+
 def slot_table(choices, num_experts):
     experts = jnp.arange(num_experts, dtype=jnp.int32)
     first_hot = (choices[..., 0:1] == experts).astype(jnp.int32)
@@ -500,7 +578,7 @@
     select = (slot_ids[:, :, None] == columns).astype(jnp.bfloat16)
 
     normed = rms_norm(hidden, ln_scale).reshape(tokens, d_model)
-    dispatched = jnp.einsum('ncs,nd->sd', select, normed, preferred_element_type=jnp.float32).astype(jnp.bfloat16)
+    dispatched = dispatch(hidden.reshape(tokens, d_model), ln_scale, slot_ids, num_experts * capacity)
     returned, *caches = moe_exchange(dispatched, expert_in, expert_out, *caches, tp, ep)
 
     logits = jnp.dot(normed.astype(jnp.float32), w_router, precision=lax.Precision.HIGHEST)
@@ -536,10 +614,8 @@
         blocks = [packed(0), w_up, w_down, packed(1), w_gate]
         hidden, tables, (attn_zero, up, down, attn_one, gate) = gather_all(hidden_in, bias_table, blocks, len(blocks) - 1, tp, ep)
         hidden, keys_zero, values_zero = attention(hidden, ln_attn[0], attn_zero, tables[0], tp)
-        keys_zero, values_zero = tp_exchange_permutes(keys_zero, tp), tp_exchange_permutes(values_zero, tp)
         hidden = dense_ffn(hidden, ln_ffn[0], gate, up, down)
-        hidden, keys_one, values_one = attention(hidden, ln_attn[1], attn_one, tables[1], tp)
-        hidden, keys_zero, values_zero = lax.optimization_barrier((hidden, keys_zero, values_zero))
+        hidden, keys_one, values_one, keys_zero, values_zero = attention(hidden, ln_attn[1], attn_one, tables[1], tp, (keys_zero, values_zero))
         hidden = lax.all_to_all(hidden, 'tp', 1, 0, tiled=True)
         hidden, keys_one, values_one = moe_block(hidden, ln_ffn[1], w_router, expert_in, expert_out, expert_ids, (keys_one, values_one), tp, ep)
         keys = jnp.stack([as_cache(keys_zero, local_heads), as_cache(keys_one, local_heads)])

time: 467 us -> 452 us (0.968)
  Pallas kernels: 304 us -> 328 us
  local copies, waits for them, and re-layouts: 47.7 us -> 27.3 us
  waiting for transfers between devices: 1.71 us -> 17.9 us
  other arithmetic: 32.9 us -> 17.7 us
  matrix products: 60.9 us -> 47.7 us
  starting transfers between devices: 11.4 us -> 4.89 us
    pallas_call x2 -> x3, Pallas kernels: 46.3 us -> 72.4 us  [the longest x2 62.9 us: attention(): pl.pallas_call(functools.partial(attention_kernel, tp, bool(old)), grid=(...]
    all_to_all x1, waiting for transfers between devices: 1.25 us -> 17.9 us  [device_fn(): hidden = lax.all_to_all(hidden, 'tp', 1, 0, tiled=True)]
    reduce_sum x1 -> x0, other arithmetic: 13.8 us -> none  [moe_block(): jnp.einsum('ncs,nd->sd', select, normed, preferred_element_type=jnp.float32)]
    dot_general x1 -> x0, matrix products: 12.3 us -> none  [moe_block(): jnp.einsum('ncs,nd->sd', select, normed, preferred_element_type=jnp.float32)]
    dynamic_update_slice x6 -> x0, local copies, waits for them, and re-layouts: 7.41 us -> none  [tp_exchange_permutes(): out = lax.dynamic_update_index_in_dim(out, got, (me + tp - step) % tp, 0)]
    ppermute x6 -> x0, starting transfers between devices: 7.31 us -> none  [tp_exchange_permutes(): got = lax.ppermute(block, 'tp', [(i, (i + step) % tp) for i in range(tp)])]
    unnamed x58 -> x46, local copies, waits for them, and re-layouts: 17.2 us -> 20 us
  transfers between devices with their start and end apart: 7 -> 1, of which waited for: 2 -> 1; matrix products, arithmetic and copies ran while one was open for 15% -> 0% of each run, Pallas kernels for 5% -> 0%
where the time goes in v3:
time: 452 us; the launch traced here: 445 us
  Pallas kernels  328 us (73%)
  matrix products  47.7 us (11%)
  local copies, waits for them, and re-layouts  27.3 us (6%)
  waiting for transfers between devices  17.9 us (4%)
  other arithmetic  17.7 us (4%)
  starting transfers between devices  4.89 us (1%)
    pallas_call x1, Pallas kernels, moe_exchange(): pl.pallas_call(functools.partial(moe_kernel, tp, ep, ff_dim // 4), in_spe...  179 us
    pallas_call x1, Pallas kernels, gather_all(): pl.pallas_call(functools.partial(gather_kernel, tp, ep, num_blocks, direc...  76.4 us
    pallas_call x2, Pallas kernels, attention(): pl.pallas_call(functools.partial(attention_kernel, tp, bool(old)), grid=(...  62.9 us
    unnamed x46, local copies, waits for them, and re-layouts  20 us
    dot_general x1, matrix products, dense_ffn(): jnp.einsum('stgf,gfd->std', ffn_hidden, down, preferred_element_type=jnp....  18.6 us
    all_to_all x1, waiting for transfers between devices, device_fn(): hidden = lax.all_to_all(hidden, 'tp', 1, 0, tiled=True)  17.9 us
    dot_general x1, matrix products, moe_block(): jnp.einsum('ncs,sd->ncd', select, returned, preferred_element_type=jnp.fl...  15.2 us
    dot_general x1, matrix products, dense_ffn(): jnp.einsum('std,gdf->stgf', normed, gate, preferred_element_type=jnp.floa...  10.6 us
  transfers between devices with their start and end apart: 1, of which 1 were waited for; matrix products, arithmetic and copies ran while one was open for 0% of the time, Pallas kernels for 0%

profile of v3, /device:TPU:97, one launch (start us, length us, event | category | flops | bytes accessed | tf_op | source)
XLA Modules:
  0.0 444.8 jit_solution(9316021857984646495)
XLA Ops:
  0.7 1.2 slice_bitcast_fusion.3
  1.8 1.1 slice_bitcast_fusion.2
  4.7 1.6 pad_maximum_fusion.2
  6.3 76.4 %gather_all.1 = (bf16[4,4,64,768]{3,2,1,0:T(8,128)(2,1)}, bf16[2,2,64,768]{3,2,1,0:T(8,128)(2,1)}, f32[4,2,3,32]{3,2,1,0:T(4,128)}, bf16[4,8,96,768]{3,2,1,0:T(8...) custom-call(bf16[4,4,64,768]{3,2,1,0:T(8,128)(2,1)} %bitcast.138, ...), custom_call_target="tpu_custom_call" | custom-call | tf_op jit(solution)/shard_map/gather_all/pallas_call | solution.py:158
  83.4 2.3 copy-done.4
  85.8 1.4 copy-done.5
  87.2 22.9 %attention.1 = (bf16[4,256,768]{2,1,0:T(8,128)(2,1)S(1)}, bf16[4,4,192,256]{3,2,1,0:T(8,128)(2,1)S(1)}, bf16[4,4,192,256]{3,2,1,0:T(8,128)(2,1)S(1)}) custom-call(bf16[4,256,768]{2,1,0:T(8,128)(2,1)S(1)} %bitcast.132, f32[1,768]{1,0:T(1,128)S(1)} %get-tuple-element.61.ln_ref, bf16[4,768,768]{2,1,0:T(8,128)(2,1)S(1)} %bitcast.131, f32[12,32]{1,0:T(8,128)S(1)} %squeeze.38.table_ref), custom_call_target="tpu_custom_call" | custom-call | flops 7247757312 | bytes 11010048 | tf_op jit(solution)/shard_map/attention/pallas_call | solution.py:309
  110.1 1.1 copy-done.11
  112.4 10.6 %fusion.26 = f32[4,256,4,768]{3,1,2,0:T(8,128)} fusion(bf16[4,768,768,1]{2,1,0,3:T(8,128)(2,1)} %bitcast.156, bf16[4,256,768]{2,1,0:T(8,128)(2,1)S(1)} %get-tuple-element.24, f32[768]{0:T(1024)S(1)} %get-tuple-element.42, f32[4,256]{1,0:T(4,128)S(1)} %add_rsqrt_fusion.1), kind=kOutput, calls=%fused_computation.31 | convolution fusion | flops 4834983936 | bytes 18881536 | tf_op jit(solution)/shard_map/std,gdf->stgf/dot_general | solution.py:325
  123.1 18.6 %fusion.16.hidden_ref = bf16[4,256,768]{2,1,0:T(8,128)(2,1)} fusion(bf16[4,256,768]{2,1,0:T(8,128)(2,1)S(1)} %get-tuple-element.24, bf16[4,768,768,1]{2,1,0,3:T(8,128)(2,1)} %bitcast.155, f32[4,256,4,768]{3,1,2,0:T(8,128)} %fusion.26, bf16[4,768,768,1]{2,1,0,3:T(8,128)(2,1)} %bitcast.154, f32[768]{0:T(1024)S(1)} %get-tuple-element.42, ...), kind=kOutput, calls=%fused_computation.21 | convolution fusion | flops 9700638720 | bytes 25172992 | tf_op jit(solution)/shard_map/stgf,gfd->std/dot_general | solution.py:328
  141.7 1.4 copy-done.10
  143.1 1.4 copy-done.12
  144.5 1.4 copy-done.13
  145.9 39.9 %attention_moving.1 = (bf16[4,256,768]{2,1,0:T(8,128)(2,1)S(1)}, bf16[4,4,192,256]{3,2,1,0:T(8,128)(2,1)S(1)}, bf16[4,4,192,256]{3,2,1,0:T(8,128)(2,1)S(1)}, bf1...) custom-call(bf16[4,256,768]{2,1,0:T(8,128)(2,1)S(1)} %copy-done.13, f32[1,768]{1,0:T(1,128)S(1)} %get-tuple-element.60.ln_ref, ...), custom_call_target="tpu_custom_call" | custom-call | flops 7247757312 | bytes 11010048 | tf_op jit(solution)/shard_map/attention_moving/pallas_call | solution.py:309
  185.9 1.2 copy-done.2
  187.1 1.1 copy-done.7
  188.2 1.1 copy-done.8
  189.4 2.4 copy.45
  191.7 4.9 %all-to-all-start = ((bf16[4,256,768]{2,0,1:T(4,128)(2,1)}), bf16[4,256,768]{2,0,1:T(4,128)(2,1)}, u32[]{:S(2)}, u32[]{:S(2)}) async-start(bf16[4,256,768]{2,0,1:T(4,128)(2,1)} %copy.45), calls=%async_computation | async-start | bytes 3145728 | tf_op jit(solution)/shard_map/all_to_all | solution.py:619
  198.5 17.9 %all-to-all-done = bf16[4,256,768]{2,0,1:T(4,128)(2,1)} async-done(((bf16[4,256,768]{2,0,1:T(4,128)(2,1)}), bf16[4,256,768]{2,0,1:T(4,128)(2,1)}, u32[]{:S(2)}, u32[]{:S(2)}) %all-to-all-start) | async-done | bytes 1572896 | tf_op jit(solution)/shard_map/all_to_all | solution.py:619
  216.4 4.1 bitcast_convert_fusion
  220.5 1.8 multiply_reduce_fusion.1
  222.3 3.2 fusion.53
  226.9 1.4 copy-done.3
  228.3 9.5 %dispatch.1 = bf16[4096,768]{1,0:T(8,128)(2,1)S(1)} custom-call(bf16[1024,768]{1,0:T(8,128)(2,1)S(1)} %bitcast.130, f32[1,768]{1,0:T(1,128)S(1)} %get-tuple-element.59.ln_ref, s32[2,1024]{1,0:T(2,128)S(1)} %fusion.59.ids_ref), custom_call_target="tpu_custom_call" | custom-call | flops 6442450944 | bytes 6291456 | tf_op jit(solution)/shard_map/dispatch/pallas_call | solution.py:545
  237.8 2.6 copy-done.6
  240.4 179.2 %moe_exchange.1 = (bf16[4,8,4,32,768]{4,3,2,1,0:T(8,128)(2,1)}, bf16[4,4,192,256]{3,2,1,0:T(8,128)(2,1)}, bf16[4,4,192,256]{3,2,1,0:T(8,128)(2,1)}, bf16[4,4,8,3...) custom-call(bf16[4,8,4,32,768]{4,3,2,1,0:T(8,128)(2,1)} %bitcast.133, bf16[4,768,3072]{2,1,0:T(8,128)(2,1)} %w_in_ref.1, ...), custom_call_target="tpu_custom_call" | custom-call | flops 38654705664 | bytes 37748736 | tf_op jit(solution)/shard_map/moe_exchange/pallas_call | solution.py:512
  419.6 4.0 pad_maximum_fusion.1
  423.6 1.9 pad_maximum_fusion
  425.6 2.0 copy-done.21
  427.5 15.2 %multiply_reduce_fusion = f32[1024,768]{1,0:T(8,128)S(1)} fusion(f32[1024,2]{0,1:T(2,128)S(1)} %broadcast_divide_fusion, bf16[4096,768,1]{1,0,2:T(8,128)(2,1)S(1)} %bitcast.157, s32[1024,2]{0,1:T(2,128)S(1)} %compare_select_fusion), kind=kOutput, calls=%fused_computation.13 | convolution fusion | flops 12895649792 | bytes 9453568 | tf_op jit(solution)/shard_map/ncs,sd->ncd/dot_general | solution.py:590
  442.7 1.6 fusion.17
  (70 shorter events, 6.8 us)
Async XLA Ops:
  0.6 221.7 %copy-start = (f32[768,128]{1,0:T(8,128)S(1)}, f32[768,128]{1,0:T(8,128)}, u32[]{:S(2)}) copy-start(f32[768,128]{1,0:T(8,128)} %param.26) | copy-start | bytes 1179652
  0.6 3.4 copy-start.16
  0.7 3.4 copy-start.20
  6.3 77.1 %copy-start.18 = (f32[2,768]{1,0:T(2,128)S(1)}, f32[2,768]{1,0:T(2,128)}, u32[]{:S(2)}) copy-start(f32[2,768]{1,0:T(2,128)} %param.16) | copy-start | bytes 18436
  83.4 2.3 copy-start.4
  85.8 1.4 copy-start.5
  87.2 24.5 %copy-start.19 = (f32[2,768]{1,0:T(2,128)S(1)}, f32[2,768]{1,0:T(2,128)}, u32[]{:S(2)}) copy-start(f32[2,768]{1,0:T(2,128)} %param.17) | copy-start | bytes 18436
  110.1 1.1 copy-start.11
  111.2 1.1 copy-start.9
  141.7 1.4 copy-start.10
  143.1 1.4 copy-start.12
  144.5 1.4 copy-start.13
  185.9 1.2 copy-start.2
  187.1 1.1 copy-start.7
  188.2 1.1 copy-start.8
  189.4 7.3 %copy-start.17 = (s32[16,64,2]{1,2,0:T(2,128)S(1)}, s32[16,64,2]{1,2,0:T(2,128)}, u32[]{:S(2)}) copy-start(s32[16,64,2]{1,2,0:T(2,128)} %param.29) | copy-start | bytes 24580
  191.7 24.7 %all-to-all-start = ((bf16[4,256,768]{2,0,1:T(4,128)(2,1)}), bf16[4,256,768]{2,0,1:T(4,128)(2,1)}, u32[]{:S(2)}, u32[]{:S(2)}) async-start(bf16[4,256,768]{2,0,1:T(4,128)(2,1)} %copy.45), calls=%async_computation | async-start | bytes 3145728 | tf_op jit(solution)/shard_map/all_to_all | solution.py:619
  226.9 1.4 copy-start.3
  237.8 2.7 copy-start.6
  419.6 4.0 copy-start.15
  423.6 3.9 copy-start.21
  427.5 15.2 %copy-start.14 = (f32[4,4,64,768]{3,2,1,0:T(8,128)S(1)}, f32[4,4,64,768]{3,2,1,0:T(8,128)}, u32[]{:S(2)}) copy-start(f32[4,4,64,768]{3,2,1,0:T(8,128)} %get-tuple-element.45) | copy-start | bytes 9437188
  442.7 1.7 copy-start.1

commit v4 on v3

--- a/solution.py
+++ b/solution.py
@@ -447,7 +447,7 @@
     out = [outward(expert) for expert in range(experts)]
     ret = [inward(expert) for expert in range(experts)]
     chain = out + ret
-    weights = {}
+    weights, own = {}, []
     last = len(chain) - 1
     chain[0].start_y()
     weights[0] = fetch(0)
@@ -469,6 +469,8 @@
         if step <= last:
             chain[step].finish_y()
             chain[step].start_x()
+            if step >= experts:
+                own.append(keep(turn_ref.at[step - experts, :, me_ep], back_ref.at[:, me_ep, step - experts]))
         if 1 <= step <= experts:
             out[step - 1].finish_x()
         if step == last - 1:
@@ -481,7 +483,6 @@
                           for index, (source, _) in enumerate(pairs) for way, peer in enumerate((to_right, to_left))]
             cache_moves = [send(source.at[goal], target.at[me_tp], peer)
                            for source, target in pairs for goal, peer in ((right, to_right), (left, to_left))]
-    own = [keep(turn_ref.at[expert, :, me_ep], back_ref.at[:, me_ep, expert]) for expert in range(experts)]
     for index, (_, target) in enumerate(pairs):
         for way, (origin, peer) in enumerate(((left, to_right), (right, to_left))):
             cache_hops[2 * index + way].wait_recv()

time: 452 us -> 452 us (level)
  no operation moved by 1% of the time
where the time goes in v4:
time: 452 us; the launch traced here: 445 us
  Pallas kernels  328 us (73%)
  matrix products  47.7 us (11%)
  local copies, waits for them, and re-layouts  27.3 us (6%)
  waiting for transfers between devices  17.9 us (4%)
  other arithmetic  17.7 us (4%)
  starting transfers between devices  4.89 us (1%)
    pallas_call x1, Pallas kernels, moe_exchange(): pl.pallas_call(functools.partial(moe_kernel, tp, ep, ff_dim // 4), in_spe...  179 us
    pallas_call x1, Pallas kernels, gather_all(): pl.pallas_call(functools.partial(gather_kernel, tp, ep, num_blocks, direc...  76.4 us
    pallas_call x2, Pallas kernels, attention(): pl.pallas_call(functools.partial(attention_kernel, tp, bool(old)), grid=(...  62.9 us
    unnamed x46, local copies, waits for them, and re-layouts  20 us
    dot_general x1, matrix products, dense_ffn(): jnp.einsum('stgf,gfd->std', ffn_hidden, down, preferred_element_type=jnp....  18.6 us
    all_to_all x1, waiting for transfers between devices, device_fn(): hidden = lax.all_to_all(hidden, 'tp', 1, 0, tiled=True)  17.9 us
    dot_general x1, matrix products, moe_block(): jnp.einsum('ncs,sd->ncd', select, returned, preferred_element_type=jnp.fl...  15.2 us
    dot_general x1, matrix products, dense_ffn(): jnp.einsum('std,gdf->stgf', normed, gate, preferred_element_type=jnp.floa...  10.6 us
  transfers between devices with their start and end apart: 1, of which 1 were waited for; matrix products, arithmetic and copies ran while one was open for 0% of the time, Pallas kernels for 0%

profile of v4, /device:TPU:97, one launch (start us, length us, event | category | flops | bytes accessed | tf_op | source)
XLA Modules:
  0.0 444.8 jit_solution(8532034399412281592)
XLA Ops:
  0.7 1.2 slice_bitcast_fusion.3
  1.8 1.1 slice_bitcast_fusion.2
  4.7 1.6 pad_maximum_fusion.2
  6.3 76.4 %gather_all.1 = (bf16[4,4,64,768]{3,2,1,0:T(8,128)(2,1)}, bf16[2,2,64,768]{3,2,1,0:T(8,128)(2,1)}, f32[4,2,3,32]{3,2,1,0:T(4,128)}, bf16[4,8,96,768]{3,2,1,0:T(8...) custom-call(bf16[4,4,64,768]{3,2,1,0:T(8,128)(2,1)} %bitcast.138, ...), custom_call_target="tpu_custom_call" | custom-call | tf_op jit(solution)/shard_map/gather_all/pallas_call | solution.py:158
  83.4 2.3 copy-done.4
  85.8 1.4 copy-done.5
  87.2 22.9 %attention.1 = (bf16[4,256,768]{2,1,0:T(8,128)(2,1)S(1)}, bf16[4,4,192,256]{3,2,1,0:T(8,128)(2,1)S(1)}, bf16[4,4,192,256]{3,2,1,0:T(8,128)(2,1)S(1)}) custom-call(bf16[4,256,768]{2,1,0:T(8,128)(2,1)S(1)} %bitcast.132, f32[1,768]{1,0:T(1,128)S(1)} %get-tuple-element.61.ln_ref, bf16[4,768,768]{2,1,0:T(8,128)(2,1)S(1)} %bitcast.131, f32[12,32]{1,0:T(8,128)S(1)} %squeeze.38.table_ref), custom_call_target="tpu_custom_call" | custom-call | flops 7247757312 | bytes 11010048 | tf_op jit(solution)/shard_map/attention/pallas_call | solution.py:309
  110.1 1.1 copy-done.11
  112.4 10.6 %fusion.26 = f32[4,256,4,768]{3,1,2,0:T(8,128)} fusion(bf16[4,768,768,1]{2,1,0,3:T(8,128)(2,1)} %bitcast.156, bf16[4,256,768]{2,1,0:T(8,128)(2,1)S(1)} %get-tuple-element.24, f32[768]{0:T(1024)S(1)} %get-tuple-element.42, f32[4,256]{1,0:T(4,128)S(1)} %add_rsqrt_fusion.1), kind=kOutput, calls=%fused_computation.31 | convolution fusion | flops 4834983936 | bytes 18881536 | tf_op jit(solution)/shard_map/std,gdf->stgf/dot_general | solution.py:325
  123.1 18.6 %fusion.16.hidden_ref = bf16[4,256,768]{2,1,0:T(8,128)(2,1)} fusion(bf16[4,256,768]{2,1,0:T(8,128)(2,1)S(1)} %get-tuple-element.24, bf16[4,768,768,1]{2,1,0,3:T(8,128)(2,1)} %bitcast.155, f32[4,256,4,768]{3,1,2,0:T(8,128)} %fusion.26, bf16[4,768,768,1]{2,1,0,3:T(8,128)(2,1)} %bitcast.154, f32[768]{0:T(1024)S(1)} %get-tuple-element.42, ...), kind=kOutput, calls=%fused_computation.21 | convolution fusion | flops 9700638720 | bytes 25172992 | tf_op jit(solution)/shard_map/stgf,gfd->std/dot_general | solution.py:328
  141.7 1.4 copy-done.10
  143.1 1.4 copy-done.12
  144.5 1.4 copy-done.13
  145.9 39.9 %attention_moving.1 = (bf16[4,256,768]{2,1,0:T(8,128)(2,1)S(1)}, bf16[4,4,192,256]{3,2,1,0:T(8,128)(2,1)S(1)}, bf16[4,4,192,256]{3,2,1,0:T(8,128)(2,1)S(1)}, bf1...) custom-call(bf16[4,256,768]{2,1,0:T(8,128)(2,1)S(1)} %copy-done.13, f32[1,768]{1,0:T(1,128)S(1)} %get-tuple-element.60.ln_ref, ...), custom_call_target="tpu_custom_call" | custom-call | flops 7247757312 | bytes 11010048 | tf_op jit(solution)/shard_map/attention_moving/pallas_call | solution.py:309
  185.9 1.2 copy-done.2
  187.1 1.1 copy-done.7
  188.2 1.1 copy-done.8
  189.4 2.4 copy.45
  191.7 4.9 %all-to-all-start = ((bf16[4,256,768]{2,0,1:T(4,128)(2,1)}), bf16[4,256,768]{2,0,1:T(4,128)(2,1)}, u32[]{:S(2)}, u32[]{:S(2)}) async-start(bf16[4,256,768]{2,0,1:T(4,128)(2,1)} %copy.45), calls=%async_computation | async-start | bytes 3145728 | tf_op jit(solution)/shard_map/all_to_all | solution.py:620
  198.5 17.9 %all-to-all-done = bf16[4,256,768]{2,0,1:T(4,128)(2,1)} async-done(((bf16[4,256,768]{2,0,1:T(4,128)(2,1)}), bf16[4,256,768]{2,0,1:T(4,128)(2,1)}, u32[]{:S(2)}, u32[]{:S(2)}) %all-to-all-start) | async-done | bytes 1572896 | tf_op jit(solution)/shard_map/all_to_all | solution.py:620
  216.4 4.1 bitcast_convert_fusion
  220.5 1.8 multiply_reduce_fusion.1
  222.3 3.2 fusion.53
  226.9 1.4 copy-done.3
  228.3 9.5 %dispatch.1 = bf16[4096,768]{1,0:T(8,128)(2,1)S(1)} custom-call(bf16[1024,768]{1,0:T(8,128)(2,1)S(1)} %bitcast.130, f32[1,768]{1,0:T(1,128)S(1)} %get-tuple-element.59.ln_ref, s32[2,1024]{1,0:T(2,128)S(1)} %fusion.59.ids_ref), custom_call_target="tpu_custom_call" | custom-call | flops 6442450944 | bytes 6291456 | tf_op jit(solution)/shard_map/dispatch/pallas_call | solution.py:546
  237.8 2.6 copy-done.6
  240.4 179.2 %moe_exchange.1 = (bf16[4,8,4,32,768]{4,3,2,1,0:T(8,128)(2,1)}, bf16[4,4,192,256]{3,2,1,0:T(8,128)(2,1)}, bf16[4,4,192,256]{3,2,1,0:T(8,128)(2,1)}, bf16[4,4,8,3...) custom-call(bf16[4,8,4,32,768]{4,3,2,1,0:T(8,128)(2,1)} %bitcast.133, bf16[4,768,3072]{2,1,0:T(8,128)(2,1)} %w_in_ref.1, ...), custom_call_target="tpu_custom_call" | custom-call | flops 38654705664 | bytes 37748736 | tf_op jit(solution)/shard_map/moe_exchange/pallas_call | solution.py:513
  419.6 4.0 pad_maximum_fusion.1
  423.6 1.9 pad_maximum_fusion
  425.6 2.0 copy-done.21
  427.5 15.2 %multiply_reduce_fusion = f32[1024,768]{1,0:T(8,128)S(1)} fusion(f32[1024,2]{0,1:T(2,128)S(1)} %broadcast_divide_fusion, bf16[4096,768,1]{1,0,2:T(8,128)(2,1)S(1)} %bitcast.157, s32[1024,2]{0,1:T(2,128)S(1)} %compare_select_fusion), kind=kOutput, calls=%fused_computation.13 | convolution fusion | flops 12895649792 | bytes 9453568 | tf_op jit(solution)/shard_map/ncs,sd->ncd/dot_general | solution.py:591
  442.7 1.6 fusion.17
  (70 shorter events, 6.8 us)
Async XLA Ops:
  0.6 221.7 %copy-start = (f32[768,128]{1,0:T(8,128)S(1)}, f32[768,128]{1,0:T(8,128)}, u32[]{:S(2)}) copy-start(f32[768,128]{1,0:T(8,128)} %param.26) | copy-start | bytes 1179652
  0.6 3.4 copy-start.16
  0.7 3.4 copy-start.20
  6.3 77.1 %copy-start.18 = (f32[2,768]{1,0:T(2,128)S(1)}, f32[2,768]{1,0:T(2,128)}, u32[]{:S(2)}) copy-start(f32[2,768]{1,0:T(2,128)} %param.16) | copy-start | bytes 18436
  83.4 2.3 copy-start.4
  85.8 1.4 copy-start.5
  87.2 24.5 %copy-start.19 = (f32[2,768]{1,0:T(2,128)S(1)}, f32[2,768]{1,0:T(2,128)}, u32[]{:S(2)}) copy-start(f32[2,768]{1,0:T(2,128)} %param.17) | copy-start | bytes 18436
  110.1 1.1 copy-start.11
  111.2 1.1 copy-start.9
  141.7 1.4 copy-start.10
  143.1 1.4 copy-start.12
  144.5 1.4 copy-start.13
  185.9 1.2 copy-start.2
  187.1 1.1 copy-start.7
  188.2 1.1 copy-start.8
  189.4 7.3 %copy-start.17 = (s32[16,64,2]{1,2,0:T(2,128)S(1)}, s32[16,64,2]{1,2,0:T(2,128)}, u32[]{:S(2)}) copy-start(s32[16,64,2]{1,2,0:T(2,128)} %param.29) | copy-start | bytes 24580
  191.7 24.7 %all-to-all-start = ((bf16[4,256,768]{2,0,1:T(4,128)(2,1)}), bf16[4,256,768]{2,0,1:T(4,128)(2,1)}, u32[]{:S(2)}, u32[]{:S(2)}) async-start(bf16[4,256,768]{2,0,1:T(4,128)(2,1)} %copy.45), calls=%async_computation | async-start | bytes 3145728 | tf_op jit(solution)/shard_map/all_to_all | solution.py:620
  226.9 1.4 copy-start.3
  237.8 2.7 copy-start.6
  419.6 4.0 copy-start.15
  423.6 3.9 copy-start.21
  427.5 15.2 %copy-start.14 = (f32[4,4,64,768]{3,2,1,0:T(8,128)S(1)}, f32[4,4,64,768]{3,2,1,0:T(8,128)}, u32[]{:S(2)}) copy-start(f32[4,4,64,768]{3,2,1,0:T(8,128)} %get-tuple-element.45) | copy-start | bytes 9437188
  442.7 1.7 copy-start.1
